TPU v7x, 32 devices: a whole 2x2x4 slice. The times are simulated.
32 devices in a mesh: gx: 4 (over z), gy: 2 (over x), gz: 4 (over y, core).
Axes of the slice: x: 2, y: 2, z: 4, core: 2. Of those that a mesh axis runs over, the one named last changes fastest.
Arguments:
- volume: bfloat16 [32, 8, 32, 512], P(None, 'gx', 'gy', 'gz'), may hold values from -6 to 6
- w_first: bfloat16 [3, 3, 3, 32, 32], replicated, may hold values from -0.21875 to 0.21875
- w_second: bfloat16 [3, 3, 3, 32, 32], replicated, may hold values from -0.21875 to 0.21875
- v_first: bfloat16 [3, 3, 3, 32, 32], replicated, may hold values from -0.21875 to 0.21875
- v_second: bfloat16 [3, 3, 3, 32, 32], replicated, may hold values from -0.21875 to 0.21875
Outputs:
- jv: bfloat16 [32, 8, 32, 512], P(None, 'gx', 'gy', 'gz')
- gv_first: float32 [3, 3, 3, 32, 32], replicated
- gv_second: float32 [3, 3, 3, 32, 32], replicated
All inputs are finite; a program needn't handle non-finite values.
Results may differ from a plain program's by a relative error of at most 0.005.
Values may be sent and summed in bfloat16 or wider, within the bound.
A program may use at most 64 MiB of HBM per device.

v0:
```python
import functools
import itertools
import math

import jax
import jax.numpy as jnp
from jax import lax
from jax.experimental import pallas as pl
from jax.experimental.pallas import tpu as pltpu
from jax.sharding import PartitionSpec as P

MESH = pl.DeviceIdType.MESH
AXES = ("gx", "gy", "gz")
STEPS = [d for d in itertools.product((-1, 0, 1), repeat=3) if d != (0, 0, 0)]
STEPS.sort(key=lambda d: (d[2] != 0, d[0] == 0, abs(d[0]) + abs(d[1])))
NT = (((1,), (1,)), ((), ()))


def gelu_pair(pre):
    inner = 0.7978845608 * (pre + 0.044715 * pre * pre * pre)
    hyper = jnp.tanh(inner)
    hidden = 0.5 * pre * (1.0 + hyper)
    slope = 0.5 * (1.0 + hyper) + 0.5 * pre * (1.0 - hyper * hyper) * 0.7978845608 * (
        1.0 + 0.134145 * pre * pre
    )
    return hidden, slope


def code(step):
    return (step[0] + 1) * 9 + (step[1] + 1) * 3 + step[2] + 1


def kernel(
    sizes,
    volume,
    w1,
    w2,
    w3,
    d1,
    d2,
    jv_out,
    gv1,
    gv2,
    *scratch,
):
    (rv, rp, rj, zv, zp, zj, ev, ep, ej, sv, sp, sj, slope_ref, back_ref,
     t1, t2, t3, shift, keep, acc, pack, land, part, full,
     hsend, hrecv, asend, arecv, bsend, brecv) = scratch
    depth, height, chan, width = volume.shape
    me = tuple(lax.axis_index(a) for a in AXES)
    total = sizes[0] * sizes[1] * sizes[2]
    line = (me[0] * sizes[1] + me[1]) * sizes[2] + me[2]

    def place(index):
        return (
            index // (sizes[1] * sizes[2]),
            index // sizes[2] % sizes[1],
            index % sizes[2],
        )

    barrier = pltpu.get_barrier_semaphore()

    @pl.loop(1, total)
    def _(i):
        pl.semaphore_signal(
            barrier, inc=1, device_id=place(lax.rem(line + i, total)), device_id_type=MESH
        )

    def there(step):
        ok = None
        for pos, size, delta in zip(me, sizes, step):
            if delta == -1:
                term = pos > 0
            elif delta == 1:
                term = pos < size - 1
            else:
                continue
            ok = term if ok is None else jnp.logical_and(ok, term)
        return ok

    def source(delta, extent):
        return {-1: pl.ds(1, 1), 1: pl.ds(extent, 1), 0: pl.ds(1, extent)}[delta]

    def target(delta, extent):
        return {-1: pl.ds(extent + 1, 1), 1: pl.ds(0, 1), 0: pl.ds(1, extent)}[delta]

    def landing(step, rows, zbuf):
        if step[2] == 0:
            return rows.at[target(step[0], depth), target(step[1], height)]
        return zbuf.at[0 if step[2] == 1 else 1, 1 - step[0], 1 - step[1]]

    def message(step, rows, zbuf, edge, slot):
        if step[2] == 0:
            src = rows.at[source(step[0], depth), source(step[1], height)]
        else:
            src = edge
        return pltpu.make_async_remote_copy(
            src_ref=src,
            dst_ref=landing(step, rows, zbuf),
            send_sem=hsend.at[slot, code(step)],
            recv_sem=hrecv.at[slot, code(step)],
            device_id=tuple(p + d for p, d in zip(me, step)),
            device_id_type=MESH,
        )

    def send(rows, zbuf, edge, slot, cross):
        for step in STEPS:
            if (step[2] != 0) == cross:

                @pl.when(there(step))
                def _():
                    message(step, rows, zbuf, edge, slot).start()

    def clear(rows, zbuf):
        for step in STEPS:
            back = tuple(-d for d in step)

            @pl.when(jnp.logical_not(there(back)))
            def _():
                ref = landing(step, rows, zbuf)
                ref[...] = jnp.zeros(ref.shape, ref.dtype)

    def receive(rows, zbuf, edge, slot, kind):
        for step in STEPS:
            if (step[0] != 0) != (kind == 1):
                continue
            back = tuple(-d for d in step)

            @pl.when(there(back))
            def _():
                message(step, rows, zbuf, edge, slot).wait_recv()

    def stage(rows, zbuf, edge, slot, out, table, group, finish):
        for kind in range(2):
            receive(rows, zbuf, edge, slot, kind)
            spread(rows, zbuf, out, (near, far)[kind])
            convolve(table, out, group, kind, finish)

    def sent(rows, zbuf, edge, slot):
        for step in STEPS:

            @pl.when(there(step))
            def _():
                message(step, rows, zbuf, edge, slot).wait_send()

    def edges(rows, edge):
        count = rows.shape[2]
        lane = lax.broadcasted_iota(jnp.int32, (count, width), 1)
        cells = depth * height
        built = jnp.zeros((count, width), jnp.float32)
        for x in range(depth):

            def step(y, built, x=x):
                row = rows[x + 1, y + 1].astype(jnp.float32)
                at = x * height + y
                built = jnp.where(lane == at, pltpu.roll(row, at, 1), built)
                return jnp.where(lane == cells + at, pltpu.roll(row, cells + at + 1, 1), built)

            built = lax.fori_loop(0, height, step, built, unroll=4)
        edge[...] = built.astype(edge.dtype)

    def shifter():
        src = lax.broadcasted_iota(jnp.int32, (2 * width, 2 * width), 0)
        dst = lax.broadcasted_iota(jnp.int32, (2 * width, 2 * width), 1)
        cells = depth * height
        low = jnp.logical_or(
            jnp.logical_and(src == dst - 1, src < width - 1),
            jnp.logical_and(
                dst == 0, jnp.logical_and(src >= width + cells, src < width + 2 * cells)
            ),
        )
        high = jnp.logical_or(
            jnp.logical_and(src == dst - width + 1, src < width),
            jnp.logical_and(
                dst == 2 * width - 1, jnp.logical_and(src >= width, src < width + cells)
            ),
        )
        pick = jnp.logical_or(
            jnp.logical_and(dst < width, low), jnp.logical_and(dst >= width, high)
        )
        shift[...] = jnp.where(pick, 1.0, 0.0).astype(shift.dtype)

    near = tuple(range(1, depth + 1))
    far = (0, depth + 1)

    def spread(rows, zbuf, out, planes):
        count = rows.shape[2]
        groups = count // chan
        lane = lax.broadcasted_iota(jnp.int32, (count, width), 1)
        cells = depth * height

        for xp in planes:
            dx = 0 if xp == 0 else (2 if xp == depth + 1 else 1)
            halo = []
            for yp in range(height + 2):
                dy = 0 if yp == 0 else (2 if yp == height + 1 else 1)
                left = zbuf[0, dx, dy].astype(jnp.float32)
                right = zbuf[1, dx, dy].astype(jnp.float32)
                at = (xp - 1) % depth * height + (yp - 1) % height
                both = jnp.where(lane == at, right, jnp.where(lane == cells + at, left, 0.0))
                halo.append(both.astype(rows.dtype))
            wide = rows[xp].reshape((height + 2) * count, width)
            lhs = jnp.concatenate([wide, jnp.concatenate(halo, axis=0)], axis=1)
            moved = jnp.dot(lhs, shift[...], preferred_element_type=jnp.float32)
            moved = moved.astype(rows.dtype).reshape(height + 2, count, 2 * width)
            kept = wide.reshape(height + 2, count, width)
            for g in range(groups):
                at = slice(g * chan, (g + 1) * chan)
                base = g * 3 * chan
                out[xp, :, base : base + chan] = moved[:, at, :width]
                out[xp, :, base + chan : base + 2 * chan] = kept[:, at]
                out[xp, :, base + 2 * chan : base + 3 * chan] = moved[:, at, width:]

    def band(weights, table, group):
        outs = weights.shape[0]
        third = weights.shape[1] // 3
        step = third // 3
        table[...] = jnp.zeros_like(table)
        for kx in range(3):
            piece = weights[:, kx * third : (kx + 1) * third]
            for ox in range(depth):
                xp = ox + kx
                kind, pos = (0, near.index(xp)) if xp in near else (1, far.index(xp))
                for oy in range(group):
                    row = (ox * group + oy) * outs
                    at = (pos * (group + 2) + oy) * step
                    table[kind, row : row + outs, at : at + third] = piece

    def convolve(table, ref, group, kind, finish):
        outs = table.shape[1] // (depth * group)
        planes = (near, far)[kind]

        @pl.loop(0, height // (2 * group))
        def _(j):
            halves = []
            for half in range(2):
                y = (2 * j + half) * group
                halves.append(
                    jnp.concatenate(
                        [
                            ref[xp, pl.ds(y, group + 2)].reshape(
                                (group + 2) * ref.shape[2], width
                            )
                            for xp in planes
                        ],
                        axis=0,
                    )
                )
            rhs = jnp.concatenate(halves, axis=1)
            out = jnp.dot(
                table[kind, :, : rhs.shape[0]], rhs, preferred_element_type=jnp.float32
            )
            if kind == 0:
                keep[j] = out
                return
            out = out + keep[j]
            for half in range(2):
                for ox in range(depth):
                    for oy in range(group):
                        row = (ox * group + oy) * outs
                        finish(
                            ox,
                            (2 * j + half) * group + oy,
                            out[row : row + outs, half * width : (half + 1) * width],
                        )

    def correlate(ref, rows, offset):
        acc[...] = jnp.zeros_like(acc)
        for x in range(depth):

            @pl.loop(0, height // 4)
            def _(j, x=x):
                y = 4 * j
                rhs = jnp.concatenate(
                    [rows[x + offset, y + i + offset] for i in range(4)], axis=1
                )
                for kx in range(3):
                    lhs = jnp.concatenate(
                        [
                            ref[x + kx, pl.ds(y + i, 3), : 3 * chan].reshape(9 * chan, width)
                            for i in range(4)
                        ],
                        axis=1,
                    )
                    acc[kx] += lax.dot_general(lhs, rhs, NT, preferred_element_type=jnp.float32)

    tiles = pack.shape[1]
    cells_all = float(depth * height * width * total)
    factor = math.sqrt(27.0 * chan)

    def owner(t):
        return t * total // tiles

    span = 8 * tiles
    lanes = width // chan

    def scatter(slot):
        for j in range(lanes):
            flat = acc[...].reshape(27 * chan, chan)
            pack[slot, :, :, j * chan : (j + 1) * chan] = flat[
                j * span : (j + 1) * span
            ].reshape(tiles, 8, chan)
        for t in range(tiles):
            at = owner(t)

            @pl.when(line != at)
            def _():
                pltpu.make_async_remote_copy(
                    src_ref=pack.at[slot, t],
                    dst_ref=land.at[slot, lax.rem(line - at + total, total) - 1],
                    send_sem=asend.at[slot],
                    recv_sem=arecv.at[slot],
                    device_id=place(at),
                    device_id_type=MESH,
                ).start()

    def gather(slot):
        for t in range(tiles):

            @pl.when(line == owner(t))
            def _():
                pltpu.make_async_copy(
                    land.at[slot], land.at[slot], arecv.at[slot]
                ).wait()
                summed = pack[slot, t] + jnp.sum(land[slot], axis=0)
                part[slot] = summed
                full[slot, t] = summed

                @pl.loop(1, total)
                def _(i):
                    pltpu.make_async_remote_copy(
                        src_ref=part.at[slot],
                        dst_ref=full.at[slot, t],
                        send_sem=bsend.at[slot],
                        recv_sem=brecv.at[slot],
                        device_id=place(lax.rem(line + i, total)),
                        device_id_type=MESH,
                    ).start()

    def owning():
        held = line == owner(0)
        for t in range(1, tiles):
            held = jnp.logical_or(held, line == owner(t))
        return held

    def drain(slot, out, direction):
        held = owning()
        for flag, count in ((held, tiles - 1), (jnp.logical_not(held), tiles)):

            @pl.when(flag)
            def _():
                some = full.at[slot, pl.ds(0, count)]
                pltpu.make_async_copy(some, some, brecv.at[slot]).wait()
                mine = pack.at[slot, pl.ds(0, count)]
                pltpu.make_async_copy(mine, mine, asend.at[slot]).wait()

        @pl.when(held)
        def _():
            pltpu.make_async_copy(land.at[slot], land.at[slot], bsend.at[slot]).wait()

        whole = full[slot].reshape(span, width)
        for j in range(lanes):
            at = slice(j * span, (j + 1) * span)
            damp = 0.1 * direction[at].astype(jnp.float32)
            out[at] = factor * (whole[:, j * chan : (j + 1) * chan] / cells_all + damp)

    inner = (slice(1, depth + 1), slice(1, height + 1))
    rv[inner] = volume[...]
    edges(rv, ev)
    for rows, zbuf in ((rv, zv), (rp, zp), (rj, zj)):
        clear(rows, zbuf)
    pl.semaphore_wait(barrier, total - 1)
    send(rv, zv, ev, 0, False)
    send(rv, zv, ev, 0, True)
    shifter()
    band(w1, t1, 2)
    band(w2, t2, 4)
    band(w3, t3, 4)

    def first(x, y, out):
        hidden, slope = gelu_pair(out[:chan])
        slope_ref[x, y] = slope
        rp[x + 1, y + 1, :chan] = hidden.astype(jnp.bfloat16)
        rp[x + 1, y + 1, chan:] = (slope * out[chan:]).astype(jnp.bfloat16)

    stage(rv, zv, ev, 0, sv, t1, 2, first)
    send(rp, zp, ep, 1, False)
    edges(rp, ep)
    send(rp, zp, ep, 1, True)

    def second(x, y, out):
        rj[x + 1, y + 1] = out.astype(jnp.bfloat16)

    stage(rp, zp, ep, 1, sp, t2, 4, second)
    send(rj, zj, ej, 2, False)
    edges(rj, ej)
    send(rj, zj, ej, 2, True)
    jv_out[...] = rj[inner]
    correlate(sp, rj, 1)
    scatter(0)

    def third(x, y, out):
        back_ref[x, y] = (slope_ref[x, y] * out).astype(jnp.bfloat16)

    stage(rj, zj, ej, 2, sj, t3, 4, third)
    gather(0)
    correlate(sv, back_ref, 0)
    scatter(1)
    gather(1)
    drain(0, gv2, d2)
    drain(1, gv1, d1)
    sent(rv, zv, ev, 0)
    sent(rp, zp, ep, 1)
    sent(rj, zj, ej, 2)


def body(volume, w_first, w_second, v_first, v_second):
    chan, depth, height, width = volume.shape
    sizes = tuple(lax.axis_size(a) for a in AXES)
    total = sizes[0] * sizes[1] * sizes[2]
    filt = 27 * chan
    tiles = filt * chan // (8 * width)
    w1 = jnp.concatenate([w_first, v_first], axis=-1).reshape(filt, 2 * chan).T
    w2 = jnp.stack([v_second, w_second], axis=2).reshape(2 * filt, chan).T
    w3 = jnp.transpose(jnp.flip(w_second, (0, 1, 2)), (3, 0, 1, 2, 4)).reshape(chan, filt)
    cells = jnp.transpose(volume, (1, 2, 0, 3))
    bf, f32 = jnp.bfloat16, jnp.float32
    pads = (depth + 2, height + 2)
    vmem = pl.BlockSpec(memory_space=pltpu.VMEM)
    jv, corr1, corr2 = pl.pallas_call(
        functools.partial(kernel, sizes),
        out_shape=(
            jax.ShapeDtypeStruct((depth, height, chan, width), bf),
            jax.ShapeDtypeStruct((filt, chan), f32),
            jax.ShapeDtypeStruct((filt, chan), f32),
        ),
        in_specs=[vmem] * 6,
        out_specs=(vmem,) * 3,
        scratch_shapes=[
            pltpu.VMEM(pads + (chan, width), bf),
            pltpu.VMEM(pads + (2 * chan, width), bf),
            pltpu.VMEM(pads + (chan, width), bf),
            pltpu.VMEM((2, 3, 3, chan, width), bf),
            pltpu.VMEM((2, 3, 3, 2 * chan, width), bf),
            pltpu.VMEM((2, 3, 3, chan, width), bf),
            pltpu.VMEM((chan, width), bf),
            pltpu.VMEM((2 * chan, width), bf),
            pltpu.VMEM((chan, width), bf),
            pltpu.VMEM(pads + (3 * chan, width), bf),
            pltpu.VMEM(pads + (6 * chan, width), bf),
            pltpu.VMEM(pads + (3 * chan, width), bf),
            pltpu.VMEM((depth, height, chan, width), f32),
            pltpu.VMEM((depth, height, chan, width), bf),
            pltpu.VMEM((2, depth * 2 * 2 * chan, depth * 4 * 3 * chan), bf),
            pltpu.VMEM((2, depth * 4 * chan, depth * 6 * 6 * chan), bf),
            pltpu.VMEM((2, depth * 4 * chan, depth * 6 * 3 * chan), bf),
            pltpu.VMEM((2 * width, 2 * width), bf),
            pltpu.VMEM((height // 4, depth * 4 * chan, 2 * width), f32),
            pltpu.VMEM((3, 9 * chan, chan), f32),
            pltpu.VMEM((2, tiles, 8, width), f32),
            pltpu.VMEM((2, total - 1, 8, width), f32),
            pltpu.VMEM((2, 8, width), f32),
            pltpu.VMEM((2, tiles, 8, width), f32),
            pltpu.SemaphoreType.DMA((3, 27)),
            pltpu.SemaphoreType.DMA((3, 27)),
            pltpu.SemaphoreType.DMA((2,)),
            pltpu.SemaphoreType.DMA((2,)),
            pltpu.SemaphoreType.DMA((2,)),
            pltpu.SemaphoreType.DMA((2,)),
        ],
        compiler_params=pltpu.CompilerParams(
            collective_id=0, has_side_effects=True, vmem_limit_bytes=48 * 1024 * 1024
        ),
    )(cells, w1, w2, w3, v_first.reshape(filt, chan), v_second.reshape(filt, chan))
    return (
        jnp.transpose(jv, (2, 0, 1, 3)),
        corr1.reshape(v_first.shape),
        corr2.reshape(v_second.shape),
    )


def solution(mesh):
    in_specs = (P(None, "gx", "gy", "gz"), P(), P(), P(), P())
    out_specs = (P(None, "gx", "gy", "gz"), P(), P())
    return jax.shard_map(body, mesh=mesh, in_specs=in_specs, out_specs=out_specs, check_vma=False)
```

profile of v0, /device:TPU:0, one launch (start us, length us, event | category | flops | bytes accessed | tf_op | source)
XLA Modules:
  0.0 58.8 jit_solution(5199614803778285124)
XLA Ops:
  0.6 1.2 %pad_maximum_fusion.1 = bf16[3,3,3,32,64]{4,3,2,1,0:T(8,128)(2,1)S(1)} fusion(bf16[3,3,3,32,32]{4,3,2,1,0:T(8,128)(2,1)} %param.8, bf16[3,3,3,32,32]{4,3,2,1,0:T(8,128)(2,1)} %param.6), kind=kLoop, calls=%fused_computation.2 | loop fusion | flops 221184 | bytes 221184 | tf_op jit(solution)/shard_map/concatenate | solution.py:423
  1.8 0.0 copy-start.2
  1.8 0.1 copy.14
  2.0 0.8 %copy-done.2 = bf16[3,3,3,32,32]{4,3,2,1,0:T(8,128)(2,1)S(1)} copy-done((bf16[3,3,3,32,32]{4,3,2,1,0:T(8,128)(2,1)S(1)}, bf16[3,3,3,32,32]{4,3,2,1,0:T(8,128)(2,1)}, u32[]{:S(2)}) %copy-start.2) | copy-done | bytes 55320
  2.8 0.2 copy.16
  2.9 0.0 copy-start.3
  2.9 0.2 reshape.29.w3
  3.1 0.7 %copy-done.3 = bf16[32,2,16,128]{3,2,1,0:T(8,128)(2,1)S(1)} copy-done((bf16[32,2,16,128]{3,2,1,0:T(8,128)(2,1)S(1)}, bf16[32,2,16,128]{3,2,1,0:T(8,128)(2,1)}, u32[]{:S(2)}) %copy-start.3) | copy-done | bytes 262168
  3.9 0.0 copy-start
  3.9 0.1 copy.19
  4.0 0.8 %copy-done = bf16[3,3,3,32,32]{4,3,2,1,0:T(8,128)(2,1)S(1)} copy-done((bf16[3,3,3,32,32]{4,3,2,1,0:T(8,128)(2,1)S(1)}, bf16[3,3,3,32,32]{4,3,2,1,0:T(8,128)(2,1)}, u32[]{:S(2)}) %copy-start) | copy-done | bytes 55320
  4.8 0.1 pad_maximum_fusion
  4.9 0.6 copy.15
  5.5 0.0 copy-start.1
  5.5 0.3 reshape.28
  5.8 0.6 %copy-done.1 = bf16[3,3,3,32,32]{4,3,2,1,0:T(8,128)(2,1)S(1)} copy-done((bf16[3,3,3,32,32]{4,3,2,1,0:T(8,128)(2,1)S(1)}, bf16[3,3,3,32,32]{4,3,2,1,0:T(8,128)(2,1)}, u32[]{:S(2)}) %copy-start.1) | copy-done | bytes 55320
  6.5 50.0 %shard_map.76 = (bf16[2,16,32,128]{3,2,1,0:T(8,128)(2,1)S(1)}, f32[864,32]{1,0:T(8,128)S(1)}, f32[864,32]{1,0:T(8,128)S(1)}) custom-call(bf16[2,16,32,128]{3,2,1,0:T(8,128)(2,1)S(1)} %bitcast.17, bf16[64,864]{1,0:T(8,128)(2,1)S(1)} %bitcast.21, bf16[32,1728]{1,0:T(8,128)(2,1)S(1)} %bitcast.22, bf16[32,864]{1,0:T(8,128)(2,1)S(1)} %reshape.29.w3, ...), custom_call_target="tpu_custom_call" | custom-call | tf_op jit(solution)/shard_map/pallas_call | solution.py:430
  56.4 0.8 %copy.17 = bf16[32,2,16,128]{3,2,1,0:T(8,128)(2,1)} copy(bf16[32,2,16,128]{3,0,2,1:T(8,128)(2,1)S(1)} %bitcast.25) | data formatting | bytes 524288
  57.3 0.8 %copy.22 = f32[3,3,3,32,32]{4,3,2,1,0:T(8,128)} copy(f32[3,3,3,32,32]{4,3,2,1,0:T(8,128)S(1)} %bitcast.24) | data formatting | bytes 221184
  58.0 0.8 %copy.23 = f32[3,3,3,32,32]{4,3,2,1,0:T(8,128)} copy(f32[3,3,3,32,32]{4,3,2,1,0:T(8,128)S(1)} %bitcast.23) | data formatting | bytes 221184
  (1 shorter events, 0.0 us)
Async XLA Ops:
  1.8 0.9 %copy-start.2 = (bf16[3,3,3,32,32]{4,3,2,1,0:T(8,128)(2,1)S(1)}, bf16[3,3,3,32,32]{4,3,2,1,0:T(8,128)(2,1)}, u32[]{:S(2)}) copy-start(bf16[3,3,3,32,32]{4,3,2,1,0:T(8,128)(2,1)} %param.7) | copy-start | bytes 165892
  2.9 1.0 %copy-start.3 = (bf16[32,2,16,128]{3,2,1,0:T(8,128)(2,1)S(1)}, bf16[32,2,16,128]{3,2,1,0:T(8,128)(2,1)}, u32[]{:S(2)}) copy-start(bf16[32,2,16,128]{3,2,1,0:T(8,128)(2,1)} %param.5) | copy-start | bytes 786436
  3.9 0.9 %copy-start = (bf16[3,3,3,32,32]{4,3,2,1,0:T(8,128)(2,1)S(1)}, bf16[3,3,3,32,32]{4,3,2,1,0:T(8,128)(2,1)}, u32[]{:S(2)}) copy-start(bf16[3,3,3,32,32]{4,3,2,1,0:T(8,128)(2,1)} %param.9) | copy-start | bytes 165892
  5.5 0.9 %copy-start.1 = (bf16[3,3,3,32,32]{4,3,2,1,0:T(8,128)(2,1)S(1)}, bf16[3,3,3,32,32]{4,3,2,1,0:T(8,128)(2,1)}, u32[]{:S(2)}) copy-start(bf16[3,3,3,32,32]{4,3,2,1,0:T(8,128)(2,1)} %param.8) | copy-start | bytes 165892
where the time goes:
time: 59 us; the launch traced here: 58.8 us
  Pallas kernels  50 us (85%)
  local copies, waits for them, and re-layouts  6.81 us (12%)
  other arithmetic  1.28 us (2%)
  between operations  0.7 us (1%)
    pallas_call x1, Pallas kernels, body(): pl.pallas_call(functools.partial(kernel, sizes), out_shape=(jax.ShapeDtyp...  50 us
    unnamed x12, local copies, waits for them, and re-layouts  5.43 us

commit v1 on v0

--- a/solution.py
+++ b/solution.py
@@ -58,14 +58,6 @@
             index % sizes[2],
         )
 
-    barrier = pltpu.get_barrier_semaphore()
-
-    @pl.loop(1, total)
-    def _(i):
-        pl.semaphore_signal(
-            barrier, inc=1, device_id=place(lax.rem(line + i, total)), device_id_type=MESH
-        )
-
     def there(step):
         ok = None
         for pos, size, delta in zip(me, sizes, step):
@@ -77,6 +69,32 @@
                 continue
             ok = term if ok is None else jnp.logical_and(ok, term)
         return ok
+
+    barrier = pltpu.get_barrier_semaphore()
+    near_only = max(sizes) <= 4
+
+    if near_only:
+        greeted = 0
+        for step in STEPS:
+            ok = there(step)
+            greeted = greeted + jnp.where(ok, 1, 0)
+
+            @pl.when(ok)
+            def _():
+                pl.semaphore_signal(
+                    barrier,
+                    inc=1,
+                    device_id=tuple(p + d for p, d in zip(me, step)),
+                    device_id_type=MESH,
+                )
+    else:
+        greeted = total - 1
+
+        @pl.loop(1, total)
+        def _(i):
+            pl.semaphore_signal(
+                barrier, inc=1, device_id=place(lax.rem(line + i, total)), device_id_type=MESH
+            )
 
     def source(delta, extent):
         return {-1: pl.ds(1, 1), 1: pl.ds(extent, 1), 0: pl.ds(1, extent)}[delta]
@@ -366,12 +384,12 @@
 
     inner = (slice(1, depth + 1), slice(1, height + 1))
     rv[inner] = volume[...]
+    pl.semaphore_wait(barrier, greeted)
+    send(rv, zv, ev, 0, False)
     edges(rv, ev)
+    send(rv, zv, ev, 0, True)
     for rows, zbuf in ((rv, zv), (rp, zp), (rj, zj)):
         clear(rows, zbuf)
-    pl.semaphore_wait(barrier, total - 1)
-    send(rv, zv, ev, 0, False)
-    send(rv, zv, ev, 0, True)
     shifter()
     band(w1, t1, 2)
     band(w2, t2, 4)
@@ -403,9 +421,9 @@
         back_ref[x, y] = (slope_ref[x, y] * out).astype(jnp.bfloat16)
 
     stage(rj, zj, ej, 2, sj, t3, 4, third)
-    gather(0)
     correlate(sv, back_ref, 0)
     scatter(1)
+    gather(0)
     gather(1)
     drain(0, gv2, d2)
     drain(1, gv1, d1)

time: 59 us -> 56.7 us (0.961)
  Pallas kernels: 50 us -> 47.7 us
    pallas_call x1, Pallas kernels: 50 us -> 47.7 us  [body(): pl.pallas_call(functools.partial(kernel, sizes), out_shape=(jax.ShapeDtyp...]
where the time goes in v1:
time: 56.7 us; the launch traced here: 56.5 us
  Pallas kernels  47.7 us (84%)
  local copies, waits for them, and re-layouts  6.81 us (12%)
  other arithmetic  1.28 us (2%)
  between operations  0.7 us (1%)
    pallas_call x1, Pallas kernels, body(): pl.pallas_call(functools.partial(kernel, sizes), out_shape=(jax.ShapeDtyp...  47.7 us
    unnamed x12, local copies, waits for them, and re-layouts  5.43 us
    concatenate x1, other arithmetic, body(): w1 = jnp.concatenate([w_first, v_first], axis=-1).reshape(filt, 2 * chan).T  1.18 us

profile of v1, /device:TPU:0, one launch (start us, length us, event | category | flops | bytes accessed | tf_op | source)
XLA Modules:
  0.0 56.5 jit_solution(16581846216404945392)
XLA Ops:
  0.6 1.2 %pad_maximum_fusion.1 = bf16[3,3,3,32,64]{4,3,2,1,0:T(8,128)(2,1)S(1)} fusion(bf16[3,3,3,32,32]{4,3,2,1,0:T(8,128)(2,1)} %param.8, bf16[3,3,3,32,32]{4,3,2,1,0:T(8,128)(2,1)} %param.6), kind=kLoop, calls=%fused_computation.2 | loop fusion | flops 221184 | bytes 221184 | tf_op jit(solution)/shard_map/concatenate | solution.py:441
  1.8 0.0 copy-start.2
  1.8 0.1 copy.14
  2.0 0.8 %copy-done.2 = bf16[3,3,3,32,32]{4,3,2,1,0:T(8,128)(2,1)S(1)} copy-done((bf16[3,3,3,32,32]{4,3,2,1,0:T(8,128)(2,1)S(1)}, bf16[3,3,3,32,32]{4,3,2,1,0:T(8,128)(2,1)}, u32[]{:S(2)}) %copy-start.2) | copy-done | bytes 55320
  2.8 0.2 copy.16
  2.9 0.0 copy-start.3
  2.9 0.2 reshape.29.w3
  3.1 0.7 %copy-done.3 = bf16[32,2,16,128]{3,2,1,0:T(8,128)(2,1)S(1)} copy-done((bf16[32,2,16,128]{3,2,1,0:T(8,128)(2,1)S(1)}, bf16[32,2,16,128]{3,2,1,0:T(8,128)(2,1)}, u32[]{:S(2)}) %copy-start.3) | copy-done | bytes 262168
  3.9 0.0 copy-start
  3.9 0.1 copy.19
  4.0 0.8 %copy-done = bf16[3,3,3,32,32]{4,3,2,1,0:T(8,128)(2,1)S(1)} copy-done((bf16[3,3,3,32,32]{4,3,2,1,0:T(8,128)(2,1)S(1)}, bf16[3,3,3,32,32]{4,3,2,1,0:T(8,128)(2,1)}, u32[]{:S(2)}) %copy-start) | copy-done | bytes 55320
  4.8 0.1 pad_maximum_fusion
  4.9 0.6 %copy.15 = bf16[3,3,2,3,32,32]{4,3,2,1,0,5:T(4,128)(2,1)S(1)} copy(bf16[3,3,2,3,32,32]{5,4,3,1,0,2:T(8,128)(2,1)S(1)} %pad_maximum_fusion) | data formatting | bytes 221184 | tf_op jit(solution)/shard_map/stack | solution.py:442
  5.5 0.0 copy-start.1
  5.5 0.3 reshape.28
  5.8 0.6 %copy-done.1 = bf16[3,3,3,32,32]{4,3,2,1,0:T(8,128)(2,1)S(1)} copy-done((bf16[3,3,3,32,32]{4,3,2,1,0:T(8,128)(2,1)S(1)}, bf16[3,3,3,32,32]{4,3,2,1,0:T(8,128)(2,1)}, u32[]{:S(2)}) %copy-start.1) | copy-done | bytes 55320
  6.5 47.7 %shard_map.76 = (bf16[2,16,32,128]{3,2,1,0:T(8,128)(2,1)S(1)}, f32[864,32]{1,0:T(8,128)S(1)}, f32[864,32]{1,0:T(8,128)S(1)}) custom-call(bf16[2,16,32,128]{3,2,1,0:T(8,128)(2,1)S(1)} %bitcast.17, bf16[64,864]{1,0:T(8,128)(2,1)S(1)} %bitcast.21, bf16[32,1728]{1,0:T(8,128)(2,1)S(1)} %bitcast.22, bf16[32,864]{1,0:T(8,128)(2,1)S(1)} %reshape.29.w3, ...), custom_call_target="tpu_custom_call" | custom-call | tf_op jit(solution)/shard_map/pallas_call | solution.py:448
  54.1 0.8 %copy.17 = bf16[32,2,16,128]{3,2,1,0:T(8,128)(2,1)} copy(bf16[32,2,16,128]{3,0,2,1:T(8,128)(2,1)S(1)} %bitcast.25) | data formatting | bytes 524288
  55.0 0.8 %copy.22 = f32[3,3,3,32,32]{4,3,2,1,0:T(8,128)} copy(f32[3,3,3,32,32]{4,3,2,1,0:T(8,128)S(1)} %bitcast.24) | data formatting | bytes 221184
  55.7 0.8 %copy.23 = f32[3,3,3,32,32]{4,3,2,1,0:T(8,128)} copy(f32[3,3,3,32,32]{4,3,2,1,0:T(8,128)S(1)} %bitcast.23) | data formatting | bytes 221184
  (1 shorter events, 0.0 us)
Async XLA Ops:
  1.8 0.9 %copy-start.2 = (bf16[3,3,3,32,32]{4,3,2,1,0:T(8,128)(2,1)S(1)}, bf16[3,3,3,32,32]{4,3,2,1,0:T(8,128)(2,1)}, u32[]{:S(2)}) copy-start(bf16[3,3,3,32,32]{4,3,2,1,0:T(8,128)(2,1)} %param.7) | copy-start | bytes 165892
  2.9 1.0 %copy-start.3 = (bf16[32,2,16,128]{3,2,1,0:T(8,128)(2,1)S(1)}, bf16[32,2,16,128]{3,2,1,0:T(8,128)(2,1)}, u32[]{:S(2)}) copy-start(bf16[32,2,16,128]{3,2,1,0:T(8,128)(2,1)} %param.5) | copy-start | bytes 786436
  3.9 0.9 %copy-start = (bf16[3,3,3,32,32]{4,3,2,1,0:T(8,128)(2,1)S(1)}, bf16[3,3,3,32,32]{4,3,2,1,0:T(8,128)(2,1)}, u32[]{:S(2)}) copy-start(bf16[3,3,3,32,32]{4,3,2,1,0:T(8,128)(2,1)} %param.9) | copy-start | bytes 165892
  5.5 0.9 %copy-start.1 = (bf16[3,3,3,32,32]{4,3,2,1,0:T(8,128)(2,1)S(1)}, bf16[3,3,3,32,32]{4,3,2,1,0:T(8,128)(2,1)}, u32[]{:S(2)}) copy-start(bf16[3,3,3,32,32]{4,3,2,1,0:T(8,128)(2,1)} %param.8) | copy-start | bytes 165892

commit v2 on v1

--- a/solution.py
+++ b/solution.py
@@ -32,12 +32,11 @@
 
 def kernel(
     sizes,
-    volume,
-    w1,
-    w2,
-    w3,
-    d1,
-    d2,
+    volume_hbm,
+    wf_hbm,
+    ws_hbm,
+    vf_hbm,
+    vs_hbm,
     jv_out,
     gv1,
     gv2,
@@ -45,8 +44,23 @@
 ):
     (rv, rp, rj, zv, zp, zj, ev, ep, ej, sv, sp, sj, slope_ref, back_ref,
      t1, t2, t3, shift, keep, acc, pack, land, part, full,
-     hsend, hrecv, asend, arecv, bsend, brecv) = scratch
-    depth, height, chan, width = volume.shape
+     hsend, hrecv, asend, arecv, bsend, brecv,
+     volume, wf, ws, vf, vs, w1, w2, w3, isem) = scratch
+    chan, depth, height, width = volume.shape
+    loads = [
+        pltpu.make_async_copy(src, dst, isem.at[i])
+        for i, (src, dst) in enumerate(
+            (
+                (volume_hbm, volume),
+                (wf_hbm, wf),
+                (ws_hbm, ws),
+                (vf_hbm, vf),
+                (vs_hbm, vs),
+            )
+        )
+    ]
+    for load in loads:
+        load.start()
     me = tuple(lax.axis_index(a) for a in AXES)
     total = sizes[0] * sizes[1] * sizes[2]
     line = (me[0] * sizes[1] + me[1]) * sizes[2] + me[2]
@@ -382,8 +396,30 @@
             damp = 0.1 * direction[at].astype(jnp.float32)
             out[at] = factor * (whole[:, j * chan : (j + 1) * chan] / cells_all + damp)
 
+    def arrange():
+        filt = 27 * chan
+        for load in loads[1:]:
+            load.wait()
+        four = jnp.concatenate([wf[...], vf[...], vs[...], ws[...]], axis=1)
+        rows = lax.broadcasted_iota(jnp.int32, (4 * chan, 4 * chan), 0)
+        cols = lax.broadcasted_iota(jnp.int32, (4 * chan, 4 * chan), 1)
+        eye = jnp.where(rows == cols, 1.0, 0.0).astype(four.dtype)
+        turned = lax.dot_general(eye, four, NT, preferred_element_type=jnp.float32)
+        turned = turned.astype(w1.dtype)
+        w1[...] = turned[: 2 * chan]
+        third = 3 * chan
+        for k in range(9):
+            part = slice(k * third, (k + 1) * third)
+            w2[:, 2 * k * third : (2 * k + 1) * third] = turned[2 * chan : 3 * chan, part]
+            w2[:, (2 * k + 1) * third : (2 * k + 2) * third] = turned[3 * chan :, part]
+        for k in range(27):
+            at = filt - (k + 1) * chan
+            w3[:, k * chan : (k + 1) * chan] = ws[at : at + chan]
+
     inner = (slice(1, depth + 1), slice(1, height + 1))
-    rv[inner] = volume[...]
+    loads[0].wait()
+    for x in range(depth):
+        rv[x + 1, 1 : height + 1] = jnp.swapaxes(volume[:, x], 0, 1)
     pl.semaphore_wait(barrier, greeted)
     send(rv, zv, ev, 0, False)
     edges(rv, ev)
@@ -391,6 +427,7 @@
     for rows, zbuf in ((rv, zv), (rp, zp), (rj, zj)):
         clear(rows, zbuf)
     shifter()
+    arrange()
     band(w1, t1, 2)
     band(w2, t2, 4)
     band(w3, t3, 4)
@@ -413,7 +450,8 @@
     send(rj, zj, ej, 2, False)
     edges(rj, ej)
     send(rj, zj, ej, 2, True)
-    jv_out[...] = rj[inner]
+    for x in range(depth):
+        jv_out[:, x] = jnp.swapaxes(rj[x + 1, 1 : height + 1], 0, 1)
     correlate(sp, rj, 1)
     scatter(0)
 
@@ -425,11 +463,23 @@
     scatter(1)
     gather(0)
     gather(1)
-    drain(0, gv2, d2)
-    drain(1, gv1, d1)
+    drain(0, gv2, vs)
+    drain(1, gv1, vf)
     sent(rv, zv, ev, 0)
     sent(rp, zp, ep, 1)
     sent(rj, zj, ej, 2)
+
+
+def place_out(*refs):
+    count = len(refs) // 2
+    sems = refs[-1]
+    copies = [
+        pltpu.make_async_copy(refs[i], refs[count + i], sems.at[i]) for i in range(count)
+    ]
+    for copy in copies:
+        copy.start()
+    for copy in copies:
+        copy.wait()
 
 
 def body(volume, w_first, w_second, v_first, v_second):
@@ -438,21 +488,17 @@
     total = sizes[0] * sizes[1] * sizes[2]
     filt = 27 * chan
     tiles = filt * chan // (8 * width)
-    w1 = jnp.concatenate([w_first, v_first], axis=-1).reshape(filt, 2 * chan).T
-    w2 = jnp.stack([v_second, w_second], axis=2).reshape(2 * filt, chan).T
-    w3 = jnp.transpose(jnp.flip(w_second, (0, 1, 2)), (3, 0, 1, 2, 4)).reshape(chan, filt)
-    cells = jnp.transpose(volume, (1, 2, 0, 3))
     bf, f32 = jnp.bfloat16, jnp.float32
     pads = (depth + 2, height + 2)
     vmem = pl.BlockSpec(memory_space=pltpu.VMEM)
     jv, corr1, corr2 = pl.pallas_call(
         functools.partial(kernel, sizes),
         out_shape=(
-            jax.ShapeDtypeStruct((depth, height, chan, width), bf),
+            jax.ShapeDtypeStruct(volume.shape, bf),
             jax.ShapeDtypeStruct((filt, chan), f32),
             jax.ShapeDtypeStruct((filt, chan), f32),
         ),
-        in_specs=[vmem] * 6,
+        in_specs=[pl.BlockSpec(memory_space=pltpu.HBM)] * 5,
         out_specs=(vmem,) * 3,
         scratch_shapes=[
             pltpu.VMEM(pads + (chan, width), bf),
@@ -485,16 +531,33 @@
             pltpu.SemaphoreType.DMA((2,)),
             pltpu.SemaphoreType.DMA((2,)),
             pltpu.SemaphoreType.DMA((2,)),
+            pltpu.VMEM(volume.shape, bf),
+            pltpu.VMEM((filt, chan), bf),
+            pltpu.VMEM((filt, chan), bf),
+            pltpu.VMEM((filt, chan), bf),
+            pltpu.VMEM((filt, chan), bf),
+            pltpu.VMEM((2 * chan, filt), bf),
+            pltpu.VMEM((chan, 2 * filt), bf),
+            pltpu.VMEM((chan, filt), bf),
+            pltpu.SemaphoreType.DMA((5,)),
         ],
         compiler_params=pltpu.CompilerParams(
             collective_id=0, has_side_effects=True, vmem_limit_bytes=48 * 1024 * 1024
         ),
-    )(cells, w1, w2, w3, v_first.reshape(filt, chan), v_second.reshape(filt, chan))
-    return (
-        jnp.transpose(jv, (2, 0, 1, 3)),
-        corr1.reshape(v_first.shape),
-        corr2.reshape(v_second.shape),
-    )
+    )(*(pltpu.with_memory_space_constraint(w, pltpu.HBM) for w in (volume, *(w.reshape(filt, chan) for w in (w_first, w_second, v_first, v_second)))))
+    jv, corr1, corr2 = pl.pallas_call(
+        place_out,
+        out_shape=(
+            jax.ShapeDtypeStruct(volume.shape, bf),
+            jax.ShapeDtypeStruct((filt, chan), f32),
+            jax.ShapeDtypeStruct((filt, chan), f32),
+        ),
+        in_specs=[vmem] * 3,
+        out_specs=(pl.BlockSpec(memory_space=pltpu.HBM),) * 3,
+        scratch_shapes=[pltpu.SemaphoreType.DMA((3,))],
+        compiler_params=pltpu.CompilerParams(vmem_limit_bytes=4 * 1024 * 1024),
+    )(jv, corr1, corr2)
+    return jv, corr1.reshape(v_first.shape), corr2.reshape(v_second.shape)
 
 
 def solution(mesh):

time: 56.7 us -> 49.7 us (0.88)
  local copies, waits for them, and re-layouts: 6.81 us -> 0 us
  Pallas kernels: 47.7 us -> 49 us
  other arithmetic: 1.28 us -> 0 us
    unnamed x12 -> x0, local copies, waits for them, and re-layouts: 5.43 us -> none
    concatenate x1 -> x0, other arithmetic: 1.18 us -> none  [body(): w1 = jnp.concatenate([w_first, v_first], axis=-1).reshape(filt, 2 * chan).T]
    pallas_call x0 -> x1, Pallas kernels: none -> 1.02 us  [body(): pl.pallas_call(place_out, out_shape=(jax.ShapeDtypeStruct(volume.shape, b...]
    reshape x3 -> x0, local copies, waits for them, and re-layouts: 0.63 us -> none  [the longest x1 0.29 us: body(): w2 = jnp.stack([v_second, w_second], axis=2).reshape(2 * filt, chan).T]
    another operation x1 -> x0, local copies, waits for them, and re-layouts: 0.58 us -> none  [body(): w2 = jnp.stack([v_second, w_second], axis=2).reshape(2 * filt, chan).T]
where the time goes in v2:
time: 49.7 us; the launch traced here: 49.6 us
  Pallas kernels  49 us (99%)
  between operations  0.64 us (1%)
    pallas_call x1, Pallas kernels, body(): pl.pallas_call(functools.partial(kernel, sizes), out_shape=(jax.ShapeDtyp...  47.9 us
    pallas_call x1, Pallas kernels, body(): pl.pallas_call(place_out, out_shape=(jax.ShapeDtypeStruct(volume.shape, b...  1.02 us

profile of v2, /device:TPU:0, one launch (start us, length us, event | category | flops | bytes accessed | tf_op | source)
XLA Modules:
  0.0 49.6 jit_solution(2196444563707121523)
XLA Ops:
  0.6 47.9 %shard_map.76 = (bf16[32,2,16,128]{3,2,1,0:T(8,128)(2,1)S(1)}, f32[864,32]{1,0:T(8,128)S(1)}, f32[864,32]{1,0:T(8,128)S(1)}) custom-call(bf16[32,2,16,128]{3,2,1,0:T(8,128)(2,1)} %volume_hbm.1, bf16[864,32]{1,0:T(8,128)(2,1)} %bitcast.6, bf16[864,32]{1,0:T(8,128)(2,1)} %bitcast.7, bf16[864,32]{1,0:T(8,128)(2,1)} %bitcast.8, bf16[864,32]{1,0:T(8,128)(2,1)} %bitcast.9), custom_call_target="tpu_custom_call" | custom-call | tf_op jit(solution)/shard_map/pallas_call | solution.py:494
  48.6 1.0 %shard_map.77 = (bf16[32,2,16,128]{3,2,1,0:T(8,128)(2,1)}, f32[864,32]{1,0:T(8,128)}, f32[864,32]{1,0:T(8,128)}) custom-call(bf16[32,2,16,128]{3,2,1,0:T(8,128)(2,1)S(1)} %get-tuple-element.9.refs_0_, f32[864,32]{1,0:T(8,128)S(1)} %get-tuple-element.10.refs_1_, f32[864,32]{1,0:T(8,128)S(1)} %get-tuple-element.11.refs_2_), custom_call_target="tpu_custom_call" | custom-call | tf_op jit(solution)/shard_map/pallas_call | solution.py:548

commit v3 on v2

--- a/solution.py
+++ b/solution.py
@@ -26,8 +26,16 @@
     return hidden, slope
 
 
-def code(step):
-    return (step[0] + 1) * 9 + (step[1] + 1) * 3 + step[2] + 1
+def codes(sizes):
+    spans = [3 if size > 2 else 2 for size in sizes]
+
+    def code(step):
+        total = 0
+        for delta, span in zip(step, spans):
+            total = total * span + (delta + 1 if span == 3 else abs(delta))
+        return total
+
+    return code, math.prod(spans)
 
 
 def kernel(
@@ -43,10 +51,11 @@
     *scratch,
 ):
     (rv, rp, rj, zv, zp, zj, ev, ep, ej, sv, sp, sj, slope_ref, back_ref,
-     t1, t2, t3, shift, keep, acc, pack, land, part, full,
+     t1, t2, t3, shift, keep, prod, diag, pack, land, part, full,
      hsend, hrecv, asend, arecv, bsend, brecv,
      volume, wf, ws, vf, vs, w1, w2, w3, isem) = scratch
     chan, depth, height, width = volume.shape
+    code, _ = codes(sizes)
     loads = [
         pltpu.make_async_copy(src, dst, isem.at[i])
         for i, (src, dst) in enumerate(
@@ -129,8 +138,8 @@
         return pltpu.make_async_remote_copy(
             src_ref=src,
             dst_ref=landing(step, rows, zbuf),
-            send_sem=hsend.at[slot, code(step)],
-            recv_sem=hrecv.at[slot, code(step)],
+            send_sem=hsend.at[code(step)],
+            recv_sem=hrecv.at[slot % 2, code(step)],
             device_id=tuple(p + d for p, d in zip(me, step)),
             device_id_type=MESH,
         )
@@ -296,99 +305,152 @@
                             out[row : row + outs, half * width : (half + 1) * width],
                         )
 
-    def correlate(ref, rows, offset):
-        acc[...] = jnp.zeros_like(acc)
-        for x in range(depth):
-
-            @pl.loop(0, height // 4)
-            def _(j, x=x):
-                y = 4 * j
-                rhs = jnp.concatenate(
-                    [rows[x + offset, y + i + offset] for i in range(4)], axis=1
-                )
-                for kx in range(3):
-                    lhs = jnp.concatenate(
-                        [
-                            ref[x + kx, pl.ds(y + i, 3), : 3 * chan].reshape(9 * chan, width)
-                            for i in range(4)
-                        ],
-                        axis=1,
-                    )
-                    acc[kx] += lax.dot_general(lhs, rhs, NT, preferred_element_type=jnp.float32)
-
     tiles = pack.shape[1]
     cells_all = float(depth * height * width * total)
     factor = math.sqrt(27.0 * chan)
-
-    def owner(t):
-        return t * total // tiles
-
     span = 8 * tiles
     lanes = width // chan
+    trio = 3 * chan
+
+    def correlate(ref, rows, offset, slot):
+        bands = range(0, height, 4)
+        lhs = jnp.concatenate(
+            [
+                ref[:, y : y + 6, :trio].reshape((depth + 2) * 6 * trio, width)
+                for y in bands
+            ],
+            axis=1,
+        )
+        inner = slice(offset, offset + depth)
+        rhs = jnp.concatenate(
+            [
+                rows[inner, y + offset : y + offset + 4].reshape(depth * 4 * chan, width)
+                for y in bands
+            ],
+            axis=1,
+        )
+        prod[...] = lax.dot_general(
+            lhs, rhs, NT, preferred_element_type=jnp.float32
+        ).reshape(prod.shape)
+
+    def fold(slot):
+        group = lax.broadcasted_iota(jnp.int32, (8, width), 1) // chan
+        for kx in range(3):
+            for r in range(0, trio, 8):
+                sums = []
+                for y in range(6):
+                    part = prod[kx, y, r : r + 8, :width]
+                    for x in range(1, depth):
+                        part = part + prod[kx + x, y, r : r + 8, x * width : (x + 1) * width]
+                    sums.append(part)
+                for ky in range(3):
+                    at = (3 * kx + ky) * trio + r
+                    keep_y = sums[ky + 3]
+                    for y in (2, 1, 0):
+                        keep_y = jnp.where(group == y, sums[ky + y], keep_y)
+                    diag[at : at + 8] = keep_y
+        low = group < 2
+        even = group % 2 == 0
+        for t in range(tiles):
+            rows = [diag[j * span + 8 * t : j * span + 8 * t + 8] for j in range(4)]
+            pairs = []
+            for j in range(2):
+                one, two = rows[j], rows[j + 2]
+                pairs.append(
+                    jnp.where(low, one, two)
+                    + pltpu.roll(jnp.where(low, two, one), 2 * chan, 1)
+                )
+            one, two = pairs
+            cross = jnp.where(even, two, one)
+            pack[slot, t] = jnp.where(even, one, two) + jnp.where(
+                even, pltpu.roll(cross, width - chan, 1), pltpu.roll(cross, chan, 1)
+            )
+
+    mids = min(2, sizes[0])
+    first_mid = (sizes[0] - mids) // 2
+    owners = mids * sizes[1] * sizes[2]
+    rounds = -(-tiles // owners)
+    is_mid = jnp.logical_and(me[0] >= first_mid, me[0] < first_mid + mids)
+    mine = (me[1] * sizes[2] + me[2]) * mids + me[0] - first_mid
+
+    def owner(t):
+        w = t % owners
+        return (first_mid + w % mids, w // mids // sizes[2], w // mids % sizes[2])
+
+    def owns(count):
+        if count == 0:
+            none = jnp.logical_or(jnp.logical_not(is_mid), mine >= tiles)
+            return none
+        more = mine + (count - 1) * owners < tiles
+        last = mine + count * owners >= tiles
+        return jnp.logical_and(is_mid, jnp.logical_and(more, last))
 
     def scatter(slot):
-        for j in range(lanes):
-            flat = acc[...].reshape(27 * chan, chan)
-            pack[slot, :, :, j * chan : (j + 1) * chan] = flat[
-                j * span : (j + 1) * span
-            ].reshape(tiles, 8, chan)
         for t in range(tiles):
-            at = owner(t)
+            spot = owner(t)
+            at = (spot[0] * sizes[1] + spot[1]) * sizes[2] + spot[2]
 
             @pl.when(line != at)
             def _():
                 pltpu.make_async_remote_copy(
                     src_ref=pack.at[slot, t],
-                    dst_ref=land.at[slot, lax.rem(line - at + total, total) - 1],
+                    dst_ref=land.at[slot, t // owners, lax.rem(line - at + total, total) - 1],
                     send_sem=asend.at[slot],
-                    recv_sem=arecv.at[slot],
-                    device_id=place(at),
+                    recv_sem=arecv.at[slot, t // owners],
+                    device_id=spot,
                     device_id_type=MESH,
                 ).start()
 
+    def others():
+        axes = [
+            [me[i] if d == 0 else lax.rem(me[i] + d, sizes[i]) for d in range(sizes[i])]
+            for i in range(3)
+        ]
+        return list(itertools.product(*axes))[1:]
+
     def gather(slot):
-        for t in range(tiles):
-
-            @pl.when(line == owner(t))
+        for r in range(rounds):
+
+            @pl.when(jnp.logical_and(is_mid, mine + r * owners < tiles))
             def _():
-                pltpu.make_async_copy(
-                    land.at[slot], land.at[slot], arecv.at[slot]
-                ).wait()
-                summed = pack[slot, t] + jnp.sum(land[slot], axis=0)
-                part[slot] = summed
+                t = mine + r * owners
+                landed = land.at[slot, r]
+                pltpu.make_async_copy(landed, landed, arecv.at[slot, r]).wait()
+                summed = pack[slot, t] + jnp.sum(land[slot, r], axis=0)
+                part[slot, r] = summed
                 full[slot, t] = summed
 
-                @pl.loop(1, total)
-                def _(i):
+                def tell(spot):
                     pltpu.make_async_remote_copy(
-                        src_ref=part.at[slot],
+                        src_ref=part.at[slot, r],
                         dst_ref=full.at[slot, t],
                         send_sem=bsend.at[slot],
                         recv_sem=brecv.at[slot],
-                        device_id=place(lax.rem(line + i, total)),
+                        device_id=spot,
                         device_id_type=MESH,
                     ).start()
 
-    def owning():
-        held = line == owner(0)
-        for t in range(1, tiles):
-            held = jnp.logical_or(held, line == owner(t))
-        return held
+                if total <= 64:
+                    for spot in others():
+                        tell(spot)
+                else:
+
+                    @pl.loop(1, total)
+                    def _(i):
+                        tell(place(lax.rem(line + i, total)))
 
     def drain(slot, out, direction):
-        held = owning()
-        for flag, count in ((held, tiles - 1), (jnp.logical_not(held), tiles)):
-
-            @pl.when(flag)
+        for count in range(rounds + 1):
+
+            @pl.when(owns(count))
             def _():
-                some = full.at[slot, pl.ds(0, count)]
+                some = full.at[slot, pl.ds(0, tiles - count)]
                 pltpu.make_async_copy(some, some, brecv.at[slot]).wait()
-                mine = pack.at[slot, pl.ds(0, count)]
-                pltpu.make_async_copy(mine, mine, asend.at[slot]).wait()
-
-        @pl.when(held)
-        def _():
-            pltpu.make_async_copy(land.at[slot], land.at[slot], bsend.at[slot]).wait()
+                sent_all = pack.at[slot, pl.ds(0, tiles - count)]
+                pltpu.make_async_copy(sent_all, sent_all, asend.at[slot]).wait()
+                if count:
+                    told = land.at[slot, pl.ds(0, count)]
+                    pltpu.make_async_copy(told, told, bsend.at[slot]).wait()
 
         whole = full[slot].reshape(span, width)
         for j in range(lanes):
@@ -439,6 +501,7 @@
         rp[x + 1, y + 1, chan:] = (slope * out[chan:]).astype(jnp.bfloat16)
 
     stage(rv, zv, ev, 0, sv, t1, 2, first)
+    sent(rv, zv, ev, 0)
     send(rp, zp, ep, 1, False)
     edges(rp, ep)
     send(rp, zp, ep, 1, True)
@@ -447,26 +510,27 @@
         rj[x + 1, y + 1] = out.astype(jnp.bfloat16)
 
     stage(rp, zp, ep, 1, sp, t2, 4, second)
+    sent(rp, zp, ep, 1)
     send(rj, zj, ej, 2, False)
     edges(rj, ej)
     send(rj, zj, ej, 2, True)
     for x in range(depth):
         jv_out[:, x] = jnp.swapaxes(rj[x + 1, 1 : height + 1], 0, 1)
-    correlate(sp, rj, 1)
+    correlate(sp, rj, 1, 0)
+    fold(0)
     scatter(0)
 
     def third(x, y, out):
         back_ref[x, y] = (slope_ref[x, y] * out).astype(jnp.bfloat16)
 
     stage(rj, zj, ej, 2, sj, t3, 4, third)
-    correlate(sv, back_ref, 0)
+    correlate(sv, back_ref, 0, 1)
+    fold(1)
     scatter(1)
     gather(0)
     gather(1)
     drain(0, gv2, vs)
     drain(1, gv1, vf)
-    sent(rv, zv, ev, 0)
-    sent(rp, zp, ep, 1)
     sent(rj, zj, ej, 2)
 
 
@@ -488,6 +552,8 @@
     total = sizes[0] * sizes[1] * sizes[2]
     filt = 27 * chan
     tiles = filt * chan // (8 * width)
+    rounds = -(-tiles // (min(2, sizes[0]) * sizes[1] * sizes[2]))
+    _, ways = codes(sizes)
     bf, f32 = jnp.bfloat16, jnp.float32
     pads = (depth + 2, height + 2)
     vmem = pl.BlockSpec(memory_space=pltpu.VMEM)
@@ -520,15 +586,16 @@
             pltpu.VMEM((2, depth * 4 * chan, depth * 6 * 3 * chan), bf),
             pltpu.VMEM((2 * width, 2 * width), bf),
             pltpu.VMEM((height // 4, depth * 4 * chan, 2 * width), f32),
-            pltpu.VMEM((3, 9 * chan, chan), f32),
+            pltpu.VMEM((depth + 2, 6, 3 * chan, depth * 4 * chan), f32),
+            pltpu.VMEM((filt, width), f32),
             pltpu.VMEM((2, tiles, 8, width), f32),
-            pltpu.VMEM((2, total - 1, 8, width), f32),
-            pltpu.VMEM((2, 8, width), f32),
+            pltpu.VMEM((2, rounds, total - 1, 8, width), f32),
+            pltpu.VMEM((2, rounds, 8, width), f32),
             pltpu.VMEM((2, tiles, 8, width), f32),
-            pltpu.SemaphoreType.DMA((3, 27)),
-            pltpu.SemaphoreType.DMA((3, 27)),
+            pltpu.SemaphoreType.DMA((ways,)),
+            pltpu.SemaphoreType.DMA((2, ways)),
             pltpu.SemaphoreType.DMA((2,)),
-            pltpu.SemaphoreType.DMA((2,)),
+            pltpu.SemaphoreType.DMA((2, rounds)),
             pltpu.SemaphoreType.DMA((2,)),
             pltpu.SemaphoreType.DMA((2,)),
             pltpu.VMEM(volume.shape, bf),

time: 49.7 us -> 45.5 us (0.915)
  Pallas kernels: 49 us -> 44.8 us
    pallas_call x1, Pallas kernels: 47.9 us -> 43.7 us  [body(): pl.pallas_call(functools.partial(kernel, sizes), out_shape=(jax.ShapeDtyp...]
where the time goes in v3:
time: 45.5 us; the launch traced here: 45.4 us
  Pallas kernels  44.8 us (98%)
  between operations  0.64 us (1%)
    pallas_call x1, Pallas kernels, body(): pl.pallas_call(functools.partial(kernel, sizes), out_shape=(jax.ShapeDtyp...  43.7 us
    pallas_call x1, Pallas kernels, body(): pl.pallas_call(place_out, out_shape=(jax.ShapeDtypeStruct(volume.shape, b...  1.02 us

profile of v3, /device:TPU:0, one launch (start us, length us, event | category | flops | bytes accessed | tf_op | source)
XLA Modules:
  0.0 45.4 jit_solution(7502897006221624917)
XLA Ops:
  0.6 43.7 %shard_map.76 = (bf16[32,2,16,128]{3,2,1,0:T(8,128)(2,1)S(1)}, f32[864,32]{1,0:T(8,128)S(1)}, f32[864,32]{1,0:T(8,128)S(1)}) custom-call(bf16[32,2,16,128]{3,2,1,0:T(8,128)(2,1)} %volume_hbm.1, bf16[864,32]{1,0:T(8,128)(2,1)} %bitcast.6, bf16[864,32]{1,0:T(8,128)(2,1)} %bitcast.7, bf16[864,32]{1,0:T(8,128)(2,1)} %bitcast.8, bf16[864,32]{1,0:T(8,128)(2,1)} %bitcast.9), custom_call_target="tpu_custom_call" | custom-call | tf_op jit(solution)/shard_map/pallas_call | solution.py:560
  44.4 1.0 %shard_map.77 = (bf16[32,2,16,128]{3,2,1,0:T(8,128)(2,1)}, f32[864,32]{1,0:T(8,128)}, f32[864,32]{1,0:T(8,128)}) custom-call(bf16[32,2,16,128]{3,2,1,0:T(8,128)(2,1)S(1)} %get-tuple-element.9.refs_0_, f32[864,32]{1,0:T(8,128)S(1)} %get-tuple-element.10.refs_1_, f32[864,32]{1,0:T(8,128)S(1)} %get-tuple-element.11.refs_2_), custom_call_target="tpu_custom_call" | custom-call | tf_op jit(solution)/shard_map/pallas_call | solution.py:615

commit v4 on v3

--- a/solution.py
+++ b/solution.py
@@ -55,7 +55,10 @@
      hsend, hrecv, asend, arecv, bsend, brecv,
      volume, wf, ws, vf, vs, w1, w2, w3, isem) = scratch
     chan, depth, height, width = volume.shape
-    code, _ = codes(sizes)
+    code, ways = codes(sizes)
+    early = height - 4
+    bands = (early - 1) // 8
+    cuts = ((height,), (4, early, height), (8 * bands, height))
     loads = [
         pltpu.make_async_copy(src, dst, isem.at[i])
         for i, (src, dst) in enumerate(
@@ -125,32 +128,57 @@
     def target(delta, extent):
         return {-1: pl.ds(extent + 1, 1), 1: pl.ds(0, 1), 0: pl.ds(1, extent)}[delta]
 
-    def landing(step, rows, zbuf):
+    def pieces(step, slot):
+        if step[1] or step[2]:
+            return [None]
+        ends = cuts[slot]
+        return [(p, lo, hi) for p, (lo, hi) in enumerate(zip((0,) + ends, ends))]
+
+    def landing(step, rows, zbuf, piece=None):
         if step[2] == 0:
-            return rows.at[target(step[0], depth), target(step[1], height)]
+            if piece is None:
+                return rows.at[target(step[0], depth), target(step[1], height)]
+            _, lo, hi = piece
+            return rows.at[target(step[0], depth), pl.ds(1 + lo, hi - lo)]
         return zbuf.at[0 if step[2] == 1 else 1, 1 - step[0], 1 - step[1]]
 
-    def message(step, rows, zbuf, edge, slot):
-        if step[2] == 0:
+    def message(step, rows, zbuf, edge, slot, piece=None):
+        lane = code(step)
+        if step[2] != 0:
+            src = edge
+        elif piece is None:
             src = rows.at[source(step[0], depth), source(step[1], height)]
         else:
-            src = edge
+            part, lo, hi = piece
+            src = rows.at[source(step[0], depth), pl.ds(1 + lo, hi - lo)]
+            if part:
+                lane = ways + 2 * (part - 1) + (step[0] > 0)
         return pltpu.make_async_remote_copy(
             src_ref=src,
-            dst_ref=landing(step, rows, zbuf),
-            send_sem=hsend.at[code(step)],
-            recv_sem=hrecv.at[slot % 2, code(step)],
+            dst_ref=landing(step, rows, zbuf, piece),
+            send_sem=hsend.at[lane],
+            recv_sem=hrecv.at[slot % 2, lane],
             device_id=tuple(p + d for p, d in zip(me, step)),
             device_id_type=MESH,
         )
 
-    def send(rows, zbuf, edge, slot, cross):
+    def send_faces(halo, part):
         for step in STEPS:
-            if (step[2] != 0) == cross:
+            found = pieces(step, halo[3])
+            if found == [None] or part >= len(found):
+                continue
+
+            @pl.when(there(step))
+            def _():
+                message(step, *halo, found[part]).start()
+
+    def send_rest(halo, cross):
+        for step in STEPS:
+            if (step[2] != 0) == cross and pieces(step, halo[3]) == [None]:
 
                 @pl.when(there(step))
                 def _():
-                    message(step, rows, zbuf, edge, slot).start()
+                    message(step, *halo).start()
 
     def clear(rows, zbuf):
         for step in STEPS:
@@ -161,41 +189,67 @@
                 ref = landing(step, rows, zbuf)
                 ref[...] = jnp.zeros(ref.shape, ref.dtype)
 
-    def receive(rows, zbuf, edge, slot, kind):
+    def receive(halo, kind, parts):
         for step in STEPS:
             if (step[0] != 0) != (kind == 1):
                 continue
+            found = pieces(step, halo[3])
+            if found == [None]:
+                found = found if 0 in parts else []
+            else:
+                found = [piece for piece in found if piece[0] in parts]
+            if not found:
+                continue
             back = tuple(-d for d in step)
 
             @pl.when(there(back))
             def _():
-                message(step, rows, zbuf, edge, slot).wait_recv()
-
-    def stage(rows, zbuf, edge, slot, out, table, group, finish):
-        for kind in range(2):
-            receive(rows, zbuf, edge, slot, kind)
-            spread(rows, zbuf, out, (near, far)[kind])
-            convolve(table, out, group, kind, finish)
-
-    def sent(rows, zbuf, edge, slot):
+                for piece in found:
+                    message(step, *halo, piece).wait_recv()
+
+    def stage(halo, out, table, group, finish, plan):
+        rows, zbuf, _, slot = halo
+        receive(halo, 0, (0,))
+        spread(rows, zbuf, out, near, 0, height + 2)
+        convolve(table, out, group, 0, finish, 0, height // (2 * group))
+        done = 0
+        for parts, upto, hook in plan:
+            if parts:
+                receive(halo, 1, parts)
+                last = cuts[slot][parts[-1]]
+                end = height + 2 if last == height else last + 1
+                start = 0 if parts[0] == 0 else cuts[slot][parts[0] - 1] + 1
+                spread(rows, zbuf, out, far, start, end)
+            convolve(table, out, group, 1, finish, done, upto)
+            done = upto
+            hook()
+
+    def sent(halo):
         for step in STEPS:
 
             @pl.when(there(step))
             def _():
-                message(step, rows, zbuf, edge, slot).wait_send()
+                for piece in pieces(step, halo[3]):
+                    message(step, *halo, piece).wait_send()
+
+    cells = depth * height
+    folds = 2 if 4 * cells <= width else 1
+    pitch = width // folds
 
     def edges(rows, edge):
-        count = rows.shape[2]
+        count = edge.shape[0]
         lane = lax.broadcasted_iota(jnp.int32, (count, width), 1)
-        cells = depth * height
         built = jnp.zeros((count, width), jnp.float32)
         for x in range(depth):
 
             def step(y, built, x=x):
-                row = rows[x + 1, y + 1].astype(jnp.float32)
-                at = x * height + y
-                built = jnp.where(lane == at, pltpu.roll(row, at, 1), built)
-                return jnp.where(lane == cells + at, pltpu.roll(row, cells + at + 1, 1), built)
+                for f in range(folds):
+                    row = rows[x + 1, y + 1, f * count : (f + 1) * count].astype(jnp.float32)
+                    at = f * pitch + x * height + y
+                    built = jnp.where(lane == at, pltpu.roll(row, at, 1), built)
+                    at = at + cells
+                    built = jnp.where(lane == at, pltpu.roll(row, at + 1, 1), built)
+                return built
 
             built = lax.fori_loop(0, height, step, built, unroll=4)
         edge[...] = built.astype(edge.dtype)
@@ -203,18 +257,18 @@
     def shifter():
         src = lax.broadcasted_iota(jnp.int32, (2 * width, 2 * width), 0)
         dst = lax.broadcasted_iota(jnp.int32, (2 * width, 2 * width), 1)
-        cells = depth * height
+        spot = src % pitch
+        right = jnp.logical_and(src >= width, spot < cells)
+        left = jnp.logical_and(
+            src >= width, jnp.logical_and(spot >= cells, spot < 2 * cells)
+        )
         low = jnp.logical_or(
             jnp.logical_and(src == dst - 1, src < width - 1),
-            jnp.logical_and(
-                dst == 0, jnp.logical_and(src >= width + cells, src < width + 2 * cells)
-            ),
+            jnp.logical_and(dst == 0, left),
         )
         high = jnp.logical_or(
             jnp.logical_and(src == dst - width + 1, src < width),
-            jnp.logical_and(
-                dst == 2 * width - 1, jnp.logical_and(src >= width, src < width + cells)
-            ),
+            jnp.logical_and(dst == 2 * width - 1, right),
         )
         pick = jnp.logical_or(
             jnp.logical_and(dst < width, low), jnp.logical_and(dst >= width, high)
@@ -224,33 +278,37 @@
     near = tuple(range(1, depth + 1))
     far = (0, depth + 1)
 
-    def spread(rows, zbuf, out, planes):
+    def spread(rows, zbuf, out, planes, start, end):
         count = rows.shape[2]
+        part = zbuf.shape[3]
         groups = count // chan
-        lane = lax.broadcasted_iota(jnp.int32, (count, width), 1)
-        cells = depth * height
+        span = end - start
+        lane = lax.broadcasted_iota(jnp.int32, (part, width), 1)
 
         for xp in planes:
             dx = 0 if xp == 0 else (2 if xp == depth + 1 else 1)
             halo = []
-            for yp in range(height + 2):
+            for yp in range(start, end):
                 dy = 0 if yp == 0 else (2 if yp == height + 1 else 1)
                 left = zbuf[0, dx, dy].astype(jnp.float32)
                 right = zbuf[1, dx, dy].astype(jnp.float32)
-                at = (xp - 1) % depth * height + (yp - 1) % height
-                both = jnp.where(lane == at, right, jnp.where(lane == cells + at, left, 0.0))
-                halo.append(both.astype(rows.dtype))
-            wide = rows[xp].reshape((height + 2) * count, width)
+                for f in range(folds):
+                    at = f * pitch + (xp - 1) % depth * height + (yp - 1) % height
+                    both = jnp.where(
+                        lane == at, right, jnp.where(lane == cells + at, left, 0.0)
+                    )
+                    halo.append(both.astype(rows.dtype))
+            wide = rows[xp, start:end].reshape(span * count, width)
             lhs = jnp.concatenate([wide, jnp.concatenate(halo, axis=0)], axis=1)
             moved = jnp.dot(lhs, shift[...], preferred_element_type=jnp.float32)
-            moved = moved.astype(rows.dtype).reshape(height + 2, count, 2 * width)
-            kept = wide.reshape(height + 2, count, width)
+            moved = moved.astype(rows.dtype).reshape(span, count, 2 * width)
+            kept = wide.reshape(span, count, width)
             for g in range(groups):
                 at = slice(g * chan, (g + 1) * chan)
                 base = g * 3 * chan
-                out[xp, :, base : base + chan] = moved[:, at, :width]
-                out[xp, :, base + chan : base + 2 * chan] = kept[:, at]
-                out[xp, :, base + 2 * chan : base + 3 * chan] = moved[:, at, width:]
+                out[xp, start:end, base : base + chan] = moved[:, at, :width]
+                out[xp, start:end, base + chan : base + 2 * chan] = kept[:, at]
+                out[xp, start:end, base + 2 * chan : base + 3 * chan] = moved[:, at, width:]
 
     def band(weights, table, group):
         outs = weights.shape[0]
@@ -267,11 +325,11 @@
                     at = (pos * (group + 2) + oy) * step
                     table[kind, row : row + outs, at : at + third] = piece
 
-    def convolve(table, ref, group, kind, finish):
+    def convolve(table, ref, group, kind, finish, lo, hi):
         outs = table.shape[1] // (depth * group)
         planes = (near, far)[kind]
 
-        @pl.loop(0, height // (2 * group))
+        @pl.loop(lo, hi)
         def _(j):
             halves = []
             for half in range(2):
@@ -482,10 +540,12 @@
     loads[0].wait()
     for x in range(depth):
         rv[x + 1, 1 : height + 1] = jnp.swapaxes(volume[:, x], 0, 1)
+    cells0, cells1, cells2 = (rv, zv, ev, 0), (rp, zp, ep, 1), (rj, zj, ej, 2)
     pl.semaphore_wait(barrier, greeted)
-    send(rv, zv, ev, 0, False)
+    send_faces(cells0, 0)
+    send_rest(cells0, False)
     edges(rv, ev)
-    send(rv, zv, ev, 0, True)
+    send_rest(cells0, True)
     for rows, zbuf in ((rv, zv), (rp, zp), (rj, zj)):
         clear(rows, zbuf)
     shifter()
@@ -500,20 +560,50 @@
         rp[x + 1, y + 1, :chan] = hidden.astype(jnp.bfloat16)
         rp[x + 1, y + 1, chan:] = (slope * out[chan:]).astype(jnp.bfloat16)
 
-    stage(rv, zv, ev, 0, sv, t1, 2, first)
-    sent(rv, zv, ev, 0)
-    send(rp, zp, ep, 1, False)
-    edges(rp, ep)
-    send(rp, zp, ep, 1, True)
+    def launch():
+        sent(cells0)
+        send_faces(cells1, 0)
+
+    def launch_rest():
+        edges(rp, ep)
+        send_rest(cells1, False)
+        send_rest(cells1, True)
+        send_faces(cells1, 2)
+
+    stage(
+        cells0,
+        sv,
+        t1,
+        2,
+        first,
+        (
+            ((0,), 1, launch),
+            ((), early // 4, lambda: send_faces(cells1, 1)),
+            ((), height // 4, launch_rest),
+        ),
+    )
 
     def second(x, y, out):
         rj[x + 1, y + 1] = out.astype(jnp.bfloat16)
 
-    stage(rp, zp, ep, 1, sp, t2, 4, second)
-    sent(rp, zp, ep, 1)
-    send(rj, zj, ej, 2, False)
-    edges(rj, ej)
-    send(rj, zj, ej, 2, True)
+    def pass_on():
+        sent(cells1)
+        send_faces(cells2, 0)
+
+    def pass_rest():
+        send_faces(cells2, 1)
+        edges(rj, ej)
+        send_rest(cells2, False)
+        send_rest(cells2, True)
+
+    stage(
+        cells1,
+        sp,
+        t2,
+        4,
+        second,
+        (((0, 1), bands, pass_on), ((2,), height // 8, pass_rest)),
+    )
     for x in range(depth):
         jv_out[:, x] = jnp.swapaxes(rj[x + 1, 1 : height + 1], 0, 1)
     correlate(sp, rj, 1, 0)
@@ -523,7 +613,7 @@
     def third(x, y, out):
         back_ref[x, y] = (slope_ref[x, y] * out).astype(jnp.bfloat16)
 
-    stage(rj, zj, ej, 2, sj, t3, 4, third)
+    stage(cells2, sj, t3, 4, third, (((0, 1), height // 8, lambda: None),))
     correlate(sv, back_ref, 0, 1)
     fold(1)
     scatter(1)
@@ -531,7 +621,7 @@
     gather(1)
     drain(0, gv2, vs)
     drain(1, gv1, vf)
-    sent(rj, zj, ej, 2)
+    sent(cells2)
 
 
 def place_out(*refs):
@@ -554,6 +644,7 @@
     tiles = filt * chan // (8 * width)
     rounds = -(-tiles // (min(2, sizes[0]) * sizes[1] * sizes[2]))
     _, ways = codes(sizes)
+    folds = 2 if 4 * depth * height <= width else 1
     bf, f32 = jnp.bfloat16, jnp.float32
     pads = (depth + 2, height + 2)
     vmem = pl.BlockSpec(memory_space=pltpu.VMEM)
@@ -570,12 +661,12 @@
             pltpu.VMEM(pads + (chan, width), bf),
             pltpu.VMEM(pads + (2 * chan, width), bf),
             pltpu.VMEM(pads + (chan, width), bf),
-            pltpu.VMEM((2, 3, 3, chan, width), bf),
-            pltpu.VMEM((2, 3, 3, 2 * chan, width), bf),
-            pltpu.VMEM((2, 3, 3, chan, width), bf),
-            pltpu.VMEM((chan, width), bf),
-            pltpu.VMEM((2 * chan, width), bf),
-            pltpu.VMEM((chan, width), bf),
+            pltpu.VMEM((2, 3, 3, chan // folds, width), bf),
+            pltpu.VMEM((2, 3, 3, 2 * chan // folds, width), bf),
+            pltpu.VMEM((2, 3, 3, chan // folds, width), bf),
+            pltpu.VMEM((chan // folds, width), bf),
+            pltpu.VMEM((2 * chan // folds, width), bf),
+            pltpu.VMEM((chan // folds, width), bf),
             pltpu.VMEM(pads + (3 * chan, width), bf),
             pltpu.VMEM(pads + (6 * chan, width), bf),
             pltpu.VMEM(pads + (3 * chan, width), bf),
@@ -592,8 +683,8 @@
             pltpu.VMEM((2, rounds, total - 1, 8, width), f32),
             pltpu.VMEM((2, rounds, 8, width), f32),
             pltpu.VMEM((2, tiles, 8, width), f32),
-            pltpu.SemaphoreType.DMA((ways,)),
-            pltpu.SemaphoreType.DMA((2, ways)),
+            pltpu.SemaphoreType.DMA((ways + 4,)),
+            pltpu.SemaphoreType.DMA((2, ways + 4)),
             pltpu.SemaphoreType.DMA((2,)),
             pltpu.SemaphoreType.DMA((2, rounds)),
             pltpu.SemaphoreType.DMA((2,)),

time: 45.5 us -> 42.4 us (0.932)
  Pallas kernels: 44.8 us -> 41.6 us
    pallas_call x1, Pallas kernels: 43.7 us -> 40.5 us  [body(): pl.pallas_call(functools.partial(kernel, sizes), out_shape=(jax.ShapeDtyp...]
where the time goes in v4:
time: 42.4 us; the launch traced here: 42.2 us
  Pallas kernels  41.6 us (98%)
  between operations  0.64 us (2%)
    pallas_call x1, Pallas kernels, body(): pl.pallas_call(functools.partial(kernel, sizes), out_shape=(jax.ShapeDtyp...  40.5 us
    pallas_call x1, Pallas kernels, body(): pl.pallas_call(place_out, out_shape=(jax.ShapeDtypeStruct(volume.shape, b...  1.02 us

profile of v4, /device:TPU:0, one launch (start us, length us, event | category | flops | bytes accessed | tf_op | source)
XLA Modules:
  0.0 42.2 jit_solution(16951961949132468089)
XLA Ops:
  0.6 40.5 %shard_map.76 = (bf16[32,2,16,128]{3,2,1,0:T(8,128)(2,1)S(1)}, f32[864,32]{1,0:T(8,128)S(1)}, f32[864,32]{1,0:T(8,128)S(1)}) custom-call(bf16[32,2,16,128]{3,2,1,0:T(8,128)(2,1)} %volume_hbm.1, bf16[864,32]{1,0:T(8,128)(2,1)} %bitcast.6, bf16[864,32]{1,0:T(8,128)(2,1)} %bitcast.7, bf16[864,32]{1,0:T(8,128)(2,1)} %bitcast.8, bf16[864,32]{1,0:T(8,128)(2,1)} %bitcast.9), custom_call_target="tpu_custom_call" | custom-call | tf_op jit(solution)/shard_map/pallas_call | solution.py:651
  41.2 1.0 %shard_map.77 = (bf16[32,2,16,128]{3,2,1,0:T(8,128)(2,1)}, f32[864,32]{1,0:T(8,128)}, f32[864,32]{1,0:T(8,128)}) custom-call(bf16[32,2,16,128]{3,2,1,0:T(8,128)(2,1)S(1)} %get-tuple-element.9.refs_0_, f32[864,32]{1,0:T(8,128)S(1)} %get-tuple-element.10.refs_1_, f32[864,32]{1,0:T(8,128)S(1)} %get-tuple-element.11.refs_2_), custom_call_target="tpu_custom_call" | custom-call | tf_op jit(solution)/shard_map/pallas_call | solution.py:706

commit v5 on v4

--- a/solution.py
+++ b/solution.py
@@ -53,12 +53,12 @@
     (rv, rp, rj, zv, zp, zj, ev, ep, ej, sv, sp, sj, slope_ref, back_ref,
      t1, t2, t3, shift, keep, prod, diag, pack, land, part, full,
      hsend, hrecv, asend, arecv, bsend, brecv,
-     volume, wf, ws, vf, vs, w1, w2, w3, isem) = scratch
+     volume, wf, ws, vf, vs, w1, w2, w3, build1, build2, isem) = scratch
     chan, depth, height, width = volume.shape
     code, ways = codes(sizes)
     early = height - 4
     bands = (early - 1) // 8
-    cuts = ((height,), (4, early, height), (8 * bands, height))
+    cuts = ((5, 9, height), (4, 8 * bands + 1, height), (8 * bands, height))
     loads = [
         pltpu.make_async_copy(src, dst, isem.at[i])
         for i, (src, dst) in enumerate(
@@ -236,23 +236,36 @@
     folds = 2 if 4 * cells <= width else 1
     pitch = width // folds
 
+    def collect(build, bits, at):
+        count = bits[0].shape[0]
+        lane = lax.broadcasted_iota(jnp.int32, (count, width), 1)
+        built = build[...]
+        for f, bit in enumerate(bits):
+            spot = f * pitch + at
+            built = jnp.where(lane == spot, pltpu.roll(bit, spot, 1), built)
+            spot = spot + cells
+            built = jnp.where(lane == spot, pltpu.roll(bit, spot + 1, 1), built)
+        build[...] = built
+
     def edges(rows, edge):
         count = edge.shape[0]
         lane = lax.broadcasted_iota(jnp.int32, (count, width), 1)
-        built = jnp.zeros((count, width), jnp.float32)
-        for x in range(depth):
-
-            def step(y, built, x=x):
-                for f in range(folds):
-                    row = rows[x + 1, y + 1, f * count : (f + 1) * count].astype(jnp.float32)
+        for f in range(folds):
+            part = slice(f * count, (f + 1) * count)
+            built = jnp.zeros((count, width), jnp.float32)
+            for x in range(depth):
+                for y in range(height):
+                    row = rows[x + 1, y + 1, part].astype(jnp.float32)
                     at = f * pitch + x * height + y
                     built = jnp.where(lane == at, pltpu.roll(row, at, 1), built)
                     at = at + cells
-                    built = jnp.where(lane == at, pltpu.roll(row, at + 1, 1), built)
-                return built
-
-            built = lax.fori_loop(0, height, step, built, unroll=4)
-        edge[...] = built.astype(edge.dtype)
+                    shift_by = (at + 1) % width
+                    built = jnp.where(lane == at, pltpu.roll(row, shift_by, 1), built)
+            if f == 0:
+                whole = built
+            else:
+                whole = jnp.where(lane < f * pitch, whole, built)
+        edge[...] = whole.astype(edge.dtype)
 
     def shifter():
         src = lax.broadcasted_iota(jnp.int32, (2 * width, 2 * width), 0)
@@ -329,7 +342,7 @@
         outs = table.shape[1] // (depth * group)
         planes = (near, far)[kind]
 
-        @pl.loop(lo, hi)
+        @pl.loop(lo, hi, unroll=hi - lo if kind == 0 and table is not t3 else 1)
         def _(j):
             halves = []
             for half in range(2):
@@ -546,6 +559,10 @@
     send_rest(cells0, False)
     edges(rv, ev)
     send_rest(cells0, True)
+    send_faces(cells0, 1)
+    send_faces(cells0, 2)
+    build1[...] = jnp.zeros_like(build1)
+    build2[...] = jnp.zeros_like(build2)
     for rows, zbuf in ((rv, zv), (rp, zp), (rj, zj)):
         clear(rows, zbuf)
     shifter()
@@ -557,15 +574,21 @@
     def first(x, y, out):
         hidden, slope = gelu_pair(out[:chan])
         slope_ref[x, y] = slope
+        tangent = slope * out[chan:]
         rp[x + 1, y + 1, :chan] = hidden.astype(jnp.bfloat16)
-        rp[x + 1, y + 1, chan:] = (slope * out[chan:]).astype(jnp.bfloat16)
+        rp[x + 1, y + 1, chan:] = tangent.astype(jnp.bfloat16)
+        if folds == 2:
+            collect(build1, (hidden, tangent), x * height + y)
 
     def launch():
         sent(cells0)
         send_faces(cells1, 0)
 
     def launch_rest():
-        edges(rp, ep)
+        if folds == 2:
+            ep[...] = build1[...].astype(ep.dtype)
+        else:
+            edges(rp, ep)
         send_rest(cells1, False)
         send_rest(cells1, True)
         send_faces(cells1, 2)
@@ -578,23 +601,30 @@
         first,
         (
             ((0,), 1, launch),
-            ((), early // 4, lambda: send_faces(cells1, 1)),
+            ((1,), 2, lambda: None),
+            ((2,), early // 4, lambda: send_faces(cells1, 1)),
             ((), height // 4, launch_rest),
         ),
     )
 
     def second(x, y, out):
         rj[x + 1, y + 1] = out.astype(jnp.bfloat16)
+        if folds == 2:
+            half = chan // 2
+            collect(build2, (out[:half], out[half:]), x * height + y)
 
     def pass_on():
         sent(cells1)
         send_faces(cells2, 0)
 
     def pass_rest():
-        send_faces(cells2, 1)
-        edges(rj, ej)
+        if folds == 2:
+            ej[...] = build2[...].astype(ej.dtype)
+        else:
+            edges(rj, ej)
         send_rest(cells2, False)
         send_rest(cells2, True)
+        send_faces(cells2, 1)
 
     stage(
         cells1,
@@ -697,6 +727,8 @@
             pltpu.VMEM((2 * chan, filt), bf),
             pltpu.VMEM((chan, 2 * filt), bf),
             pltpu.VMEM((chan, filt), bf),
+            pltpu.VMEM((2 * chan // folds, width), f32),
+            pltpu.VMEM((chan // folds, width), f32),
             pltpu.SemaphoreType.DMA((5,)),
         ],
         compiler_params=pltpu.CompilerParams(

time: 42.4 us -> 40.1 us (0.946)
  Pallas kernels: 41.6 us -> 39.3 us
    pallas_call x1, Pallas kernels: 40.5 us -> 38.3 us  [body(): pl.pallas_call(functools.partial(kernel, sizes), out_shape=(jax.ShapeDtyp...]
where the time goes in v5:
time: 40.1 us; the launch traced here: 40 us
  Pallas kernels  39.3 us (98%)
  between operations  0.64 us (2%)
    pallas_call x1, Pallas kernels, body(): pl.pallas_call(functools.partial(kernel, sizes), out_shape=(jax.ShapeDtyp...  38.3 us
    pallas_call x1, Pallas kernels, body(): pl.pallas_call(place_out, out_shape=(jax.ShapeDtypeStruct(volume.shape, b...  1.02 us

profile of v5, /device:TPU:0, one launch (start us, length us, event | category | flops | bytes accessed | tf_op | source)
XLA Modules:
  0.0 40.0 jit_solution(16462091582455434393)
XLA Ops:
  0.6 38.3 %shard_map.76 = (bf16[32,2,16,128]{3,2,1,0:T(8,128)(2,1)S(1)}, f32[864,32]{1,0:T(8,128)S(1)}, f32[864,32]{1,0:T(8,128)S(1)}) custom-call(bf16[32,2,16,128]{3,2,1,0:T(8,128)(2,1)} %volume_hbm.1, bf16[864,32]{1,0:T(8,128)(2,1)} %bitcast.6, bf16[864,32]{1,0:T(8,128)(2,1)} %bitcast.7, bf16[864,32]{1,0:T(8,128)(2,1)} %bitcast.8, bf16[864,32]{1,0:T(8,128)(2,1)} %bitcast.9), custom_call_target="tpu_custom_call" | custom-call | tf_op jit(solution)/shard_map/pallas_call | solution.py:681
  39.0 1.0 %shard_map.77 = (bf16[32,2,16,128]{3,2,1,0:T(8,128)(2,1)}, f32[864,32]{1,0:T(8,128)}, f32[864,32]{1,0:T(8,128)}) custom-call(bf16[32,2,16,128]{3,2,1,0:T(8,128)(2,1)S(1)} %get-tuple-element.9.refs_0_, f32[864,32]{1,0:T(8,128)S(1)} %get-tuple-element.10.refs_1_, f32[864,32]{1,0:T(8,128)S(1)} %get-tuple-element.11.refs_2_), custom_call_target="tpu_custom_call" | custom-call | tf_op jit(solution)/shard_map/pallas_call | solution.py:738

commit v6 on v5

--- a/solution.py
+++ b/solution.py
@@ -36,6 +36,20 @@
         return total
 
     return code, math.prod(spans)
+
+
+def owners(sizes):
+    mids = min(2, sizes[0])
+    start = (sizes[0] - mids) // 2
+    spots = [
+        (x, y, z)
+        for z in range(sizes[2])
+        for y in range(sizes[1])
+        for x in range(start, start + mids)
+    ]
+    base = [spot for spot in spots if spot[2] % 2 == 1][:8]
+    rest = [spot for spot in spots if spot not in base]
+    return base, [rest[0], rest[-1], rest[len(rest) // 2 - 1]]
 
 
 def kernel(
@@ -51,7 +65,7 @@
     *scratch,
 ):
     (rv, rp, rj, zv, zp, zj, ev, ep, ej, sv, sp, sj, slope_ref, back_ref,
-     t1, t2, t3, shift, keep, prod, diag, pack, land, part, full,
+     t1, t2, t3, shift, keep, prod, diag, pack, land, part, full, told,
      hsend, hrecv, asend, arecv, bsend, brecv,
      volume, wf, ws, vf, vs, w1, w2, w3, build1, build2, isem) = scratch
     chan, depth, height, width = volume.shape
@@ -379,51 +393,58 @@
     tiles = pack.shape[1]
     cells_all = float(depth * height * width * total)
     factor = math.sqrt(27.0 * chan)
-    span = 8 * tiles
     lanes = width // chan
     trio = 3 * chan
 
     def correlate(ref, rows, offset, slot):
-        bands = range(0, height, 4)
-        lhs = jnp.concatenate(
-            [
-                ref[:, y : y + 6, :trio].reshape((depth + 2) * 6 * trio, width)
-                for y in bands
-            ],
-            axis=1,
-        )
+        starts_y = range(0, height, 4)
         inner = slice(offset, offset + depth)
         rhs = jnp.concatenate(
             [
                 rows[inner, y + offset : y + offset + 4].reshape(depth * 4 * chan, width)
-                for y in bands
+                for y in starts_y
             ],
             axis=1,
         )
-        prod[...] = lax.dot_general(
-            lhs, rhs, NT, preferred_element_type=jnp.float32
-        ).reshape(prod.shape)
-
-    def fold(slot):
+
+        def multiply(planes):
+            lhs = jnp.concatenate(
+                [ref[planes, y : y + 6, :trio].reshape(-1, width) for y in starts_y], axis=1
+            )
+            prod[planes] = lax.dot_general(
+                lhs, rhs, NT, preferred_element_type=jnp.float32
+            ).reshape((-1,) + prod.shape[1:])
+
+        multiply(slice(0, depth + 2))
+        for kx in range(3):
+            fold(kx, slot)
+            scatter(kx, slot)
+
+    slab = 9 * chan
+    step_rows = slab // lanes
+    batch = step_rows // 8
+
+    def fold(kx, slot):
         group = lax.broadcasted_iota(jnp.int32, (8, width), 1) // chan
-        for kx in range(3):
-            for r in range(0, trio, 8):
-                sums = []
-                for y in range(6):
-                    part = prod[kx, y, r : r + 8, :width]
-                    for x in range(1, depth):
-                        part = part + prod[kx + x, y, r : r + 8, x * width : (x + 1) * width]
-                    sums.append(part)
-                for ky in range(3):
-                    at = (3 * kx + ky) * trio + r
-                    keep_y = sums[ky + 3]
-                    for y in (2, 1, 0):
-                        keep_y = jnp.where(group == y, sums[ky + y], keep_y)
-                    diag[at : at + 8] = keep_y
+        for r in range(0, trio, 8):
+            sums = []
+            for y in range(6):
+                part_sum = prod[kx, y, r : r + 8, :width]
+                for x in range(1, depth):
+                    part_sum = part_sum + prod[
+                        kx + x, y, r : r + 8, x * width : (x + 1) * width
+                    ]
+                sums.append(part_sum)
+            for ky in range(3):
+                at = ky * trio + r
+                keep_y = sums[ky + 3]
+                for y in (2, 1, 0):
+                    keep_y = jnp.where(group == y, sums[ky + y], keep_y)
+                diag[at : at + 8] = keep_y
         low = group < 2
         even = group % 2 == 0
-        for t in range(tiles):
-            rows = [diag[j * span + 8 * t : j * span + 8 * t + 8] for j in range(4)]
+        for i in range(batch):
+            rows = [diag[j * step_rows + 8 * i : j * step_rows + 8 * i + 8] for j in range(4)]
             pairs = []
             for j in range(2):
                 one, two = rows[j], rows[j + 2]
@@ -433,44 +454,46 @@
                 )
             one, two = pairs
             cross = jnp.where(even, two, one)
-            pack[slot, t] = jnp.where(even, one, two) + jnp.where(
+            pack[slot, kx * batch + i] = jnp.where(even, one, two) + jnp.where(
                 even, pltpu.roll(cross, width - chan, 1), pltpu.roll(cross, chan, 1)
             )
 
-    mids = min(2, sizes[0])
-    first_mid = (sizes[0] - mids) // 2
-    owners = mids * sizes[1] * sizes[2]
-    rounds = -(-tiles // owners)
-    is_mid = jnp.logical_and(me[0] >= first_mid, me[0] < first_mid + mids)
-    mine = (me[1] * sizes[2] + me[2]) * mids + me[0] - first_mid
-
-    def owner(t):
-        w = t % owners
-        return (first_mid + w % mids, w // mids // sizes[2], w // mids % sizes[2])
-
-    def owns(count):
-        if count == 0:
-            none = jnp.logical_or(jnp.logical_not(is_mid), mine >= tiles)
-            return none
-        more = mine + (count - 1) * owners < tiles
-        last = mine + count * owners >= tiles
-        return jnp.logical_and(is_mid, jnp.logical_and(more, last))
-
-    def scatter(slot):
-        for t in range(tiles):
-            spot = owner(t)
-            at = (spot[0] * sizes[1] + spot[1]) * sizes[2] + spot[2]
-
-            @pl.when(line != at)
-            def _():
-                pltpu.make_async_remote_copy(
-                    src_ref=pack.at[slot, t],
-                    dst_ref=land.at[slot, t // owners, lax.rem(line - at + total, total) - 1],
-                    send_sem=asend.at[slot],
-                    recv_sem=arecv.at[slot, t // owners],
-                    device_id=spot,
-                    device_id_type=MESH,
-                ).start()
+    base, extra = owners(sizes)
+
+    def at_spot(spot):
+        return jnp.logical_and(
+            me[0] == spot[0], jnp.logical_and(me[1] == spot[1], me[2] == spot[2])
+        )
+
+    def which(spots):
+        found, index = False, 0
+        for i, spot in enumerate(spots):
+            here = at_spot(spot)
+            found = jnp.logical_or(found, here)
+            index = index + jnp.where(here, i, 0)
+        return found, index
+
+    is_base, base_at = which(base)
+    is_extra, extra_at = which(extra)
+
+    def give(slot, t, chunk, spot):
+        at = (spot[0] * sizes[1] + spot[1]) * sizes[2] + spot[2]
+
+        @pl.when(line != at)
+        def _():
+            pltpu.make_async_remote_copy(
+                src_ref=pack.at[slot, t],
+                dst_ref=land.at[slot, chunk, lax.rem(line - at + total, total) - 1],
+                send_sem=asend.at[slot],
+                recv_sem=arecv.at[slot, chunk],
+                device_id=spot,
+                device_id_type=MESH,
+            ).start()
+
+    def scatter(kx, slot):
+        for w, spot in enumerate(base):
+            give(slot, kx * batch + w, kx, spot)
+        give(slot, kx * batch + len(base), 0, extra[kx])
 
     def others():
         axes = [
@@ -479,55 +502,63 @@
         ]
         return list(itertools.product(*axes))[1:]
 
+    def finish_tile(slot, t, chunk, row, column):
+        landed = land.at[slot, chunk]
+        pltpu.make_async_copy(landed, landed, arecv.at[slot, chunk]).wait()
+        rounded = (pack[slot, t] + jnp.sum(land[slot, chunk], axis=0)).astype(part.dtype)
+        part[slot, chunk] = rounded
+        full[slot, row, column] = rounded
+
+        def tell(spot):
+            pltpu.make_async_remote_copy(
+                src_ref=part.at[slot, chunk],
+                dst_ref=full.at[slot, row, column],
+                send_sem=bsend.at[slot],
+                recv_sem=brecv.at[slot],
+                device_id=spot,
+                device_id_type=MESH,
+            ).start()
+
+        if total <= 64:
+            for spot in others():
+                tell(spot)
+        else:
+
+            @pl.loop(1, total)
+            def _(i):
+                tell(place(lax.rem(line + i, total)))
+
     def gather(slot):
-        for r in range(rounds):
-
-            @pl.when(jnp.logical_and(is_mid, mine + r * owners < tiles))
+        @pl.when(is_base)
+        def _():
+            for kx in range(3):
+                finish_tile(slot, kx * batch + base_at, kx, base_at, kx)
+
+        @pl.when(is_extra)
+        def _():
+            finish_tile(slot, extra_at * batch + len(base), 0, len(base), extra_at)
+
+    def drain(slot, out, direction):
+        none = jnp.logical_not(jnp.logical_or(is_base, is_extra))
+        for owned, here in ((3, is_base), (1, is_extra), (0, none)):
+
+            @pl.when(here)
             def _():
-                t = mine + r * owners
-                landed = land.at[slot, r]
-                pltpu.make_async_copy(landed, landed, arecv.at[slot, r]).wait()
-                summed = pack[slot, t] + jnp.sum(land[slot, r], axis=0)
-                part[slot, r] = summed
-                full[slot, t] = summed
-
-                def tell(spot):
-                    pltpu.make_async_remote_copy(
-                        src_ref=part.at[slot, r],
-                        dst_ref=full.at[slot, t],
-                        send_sem=bsend.at[slot],
-                        recv_sem=brecv.at[slot],
-                        device_id=spot,
-                        device_id_type=MESH,
-                    ).start()
-
-                if total <= 64:
-                    for spot in others():
-                        tell(spot)
-                else:
-
-                    @pl.loop(1, total)
-                    def _(i):
-                        tell(place(lax.rem(line + i, total)))
-
-    def drain(slot, out, direction):
-        for count in range(rounds + 1):
-
-            @pl.when(owns(count))
-            def _():
-                some = full.at[slot, pl.ds(0, tiles - count)]
+                some = told.at[pl.ds(0, tiles - owned)]
                 pltpu.make_async_copy(some, some, brecv.at[slot]).wait()
-                sent_all = pack.at[slot, pl.ds(0, tiles - count)]
+                sent_all = pack.at[slot, pl.ds(0, tiles - owned)]
                 pltpu.make_async_copy(sent_all, sent_all, asend.at[slot]).wait()
-                if count:
-                    told = land.at[slot, pl.ds(0, count)]
-                    pltpu.make_async_copy(told, told, bsend.at[slot]).wait()
-
-        whole = full[slot].reshape(span, width)
-        for j in range(lanes):
-            at = slice(j * span, (j + 1) * span)
-            damp = 0.1 * direction[at].astype(jnp.float32)
-            out[at] = factor * (whole[:, j * chan : (j + 1) * chan] / cells_all + damp)
+                if owned:
+                    gone = told.at[pl.ds(0, owned * (total - 1))]
+                    pltpu.make_async_copy(gone, gone, bsend.at[slot]).wait()
+
+        for kx in range(3):
+            whole = full[slot, :, kx].astype(jnp.float32).reshape(step_rows, width)
+            for j in range(lanes):
+                at = slice(kx * slab + j * step_rows, kx * slab + (j + 1) * step_rows)
+                damp = 0.1 * direction[at].astype(jnp.float32)
+                mean = whole[:, j * chan : (j + 1) * chan] * (1.0 / cells_all)
+                out[at] = factor * (mean + damp)
 
     def arrange():
         filt = 27 * chan
@@ -637,16 +668,12 @@
     for x in range(depth):
         jv_out[:, x] = jnp.swapaxes(rj[x + 1, 1 : height + 1], 0, 1)
     correlate(sp, rj, 1, 0)
-    fold(0)
-    scatter(0)
 
     def third(x, y, out):
         back_ref[x, y] = (slope_ref[x, y] * out).astype(jnp.bfloat16)
 
     stage(cells2, sj, t3, 4, third, (((0, 1), height // 8, lambda: None),))
     correlate(sv, back_ref, 0, 1)
-    fold(1)
-    scatter(1)
     gather(0)
     gather(1)
     drain(0, gv2, vs)
@@ -672,7 +699,6 @@
     total = sizes[0] * sizes[1] * sizes[2]
     filt = 27 * chan
     tiles = filt * chan // (8 * width)
-    rounds = -(-tiles // (min(2, sizes[0]) * sizes[1] * sizes[2]))
     _, ways = codes(sizes)
     folds = 2 if 4 * depth * height <= width else 1
     bf, f32 = jnp.bfloat16, jnp.float32
@@ -708,15 +734,16 @@
             pltpu.VMEM((2 * width, 2 * width), bf),
             pltpu.VMEM((height // 4, depth * 4 * chan, 2 * width), f32),
             pltpu.VMEM((depth + 2, 6, 3 * chan, depth * 4 * chan), f32),
-            pltpu.VMEM((filt, width), f32),
+            pltpu.VMEM((9 * chan, width), f32),
             pltpu.VMEM((2, tiles, 8, width), f32),
-            pltpu.VMEM((2, rounds, total - 1, 8, width), f32),
-            pltpu.VMEM((2, rounds, 8, width), f32),
-            pltpu.VMEM((2, tiles, 8, width), f32),
+            pltpu.VMEM((2, 3, total - 1, 8, width), f32),
+            pltpu.VMEM((2, 3, 8, width), bf),
+            pltpu.VMEM((2, 9, 3, 8, width), bf),
+            pltpu.VMEM(((total - 1) * 3, 8, width), bf),
             pltpu.SemaphoreType.DMA((ways + 4,)),
             pltpu.SemaphoreType.DMA((2, ways + 4)),
             pltpu.SemaphoreType.DMA((2,)),
-            pltpu.SemaphoreType.DMA((2, rounds)),
+            pltpu.SemaphoreType.DMA((2, 3)),
             pltpu.SemaphoreType.DMA((2,)),
             pltpu.SemaphoreType.DMA((2,)),
             pltpu.VMEM(volume.shape, bf),

time: 40.1 us -> 39.4 us (0.983)
  Pallas kernels: 39.3 us -> 38.6 us
    pallas_call x1, Pallas kernels: 38.3 us -> 37.5 us  [body(): pl.pallas_call(functools.partial(kernel, sizes), out_shape=(jax.ShapeDtyp...]
where the time goes in v6:
time: 39.4 us; the launch traced here: 39.2 us
  Pallas kernels  38.6 us (98%)
  between operations  0.64 us (2%)
    pallas_call x1, Pallas kernels, body(): pl.pallas_call(functools.partial(kernel, sizes), out_shape=(jax.ShapeDtyp...  37.5 us
    pallas_call x1, Pallas kernels, body(): pl.pallas_call(place_out, out_shape=(jax.ShapeDtypeStruct(volume.shape, b...  1.02 us

profile of v6, /device:TPU:0, one launch (start us, length us, event | category | flops | bytes accessed | tf_op | source)
XLA Modules:
  0.0 39.2 jit_solution(1626350970379827014)
XLA Ops:
  0.6 37.5 %shard_map.76 = (bf16[32,2,16,128]{3,2,1,0:T(8,128)(2,1)S(1)}, f32[864,32]{1,0:T(8,128)S(1)}, f32[864,32]{1,0:T(8,128)S(1)}) custom-call(bf16[32,2,16,128]{3,2,1,0:T(8,128)(2,1)} %volume_hbm.1, bf16[864,32]{1,0:T(8,128)(2,1)} %bitcast.6, bf16[864,32]{1,0:T(8,128)(2,1)} %bitcast.7, bf16[864,32]{1,0:T(8,128)(2,1)} %bitcast.8, bf16[864,32]{1,0:T(8,128)(2,1)} %bitcast.9), custom_call_target="tpu_custom_call" | custom-call | tf_op jit(solution)/shard_map/pallas_call | solution.py:707
  38.2 1.0 %shard_map.77 = (bf16[32,2,16,128]{3,2,1,0:T(8,128)(2,1)}, f32[864,32]{1,0:T(8,128)}, f32[864,32]{1,0:T(8,128)}) custom-call(bf16[32,2,16,128]{3,2,1,0:T(8,128)(2,1)S(1)} %get-tuple-element.9.refs_0_, f32[864,32]{1,0:T(8,128)S(1)} %get-tuple-element.10.refs_1_, f32[864,32]{1,0:T(8,128)S(1)} %get-tuple-element.11.refs_2_), custom_call_target="tpu_custom_call" | custom-call | tf_op jit(solution)/shard_map/pallas_call | solution.py:765

commit v7 on v6

--- a/solution.py
+++ b/solution.py
@@ -252,43 +252,37 @@
 
     def collect(build, bits, at):
         count = bits[0].shape[0]
-        lane = lax.broadcasted_iota(jnp.int32, (count, width), 1)
+        pair = lax.broadcasted_iota(jnp.int32, (count, width), 1) // 2
         built = build[...]
         for f, bit in enumerate(bits):
-            spot = f * pitch + at
-            built = jnp.where(lane == spot, pltpu.roll(bit, spot, 1), built)
-            spot = spot + cells
-            built = jnp.where(lane == spot, pltpu.roll(bit, spot + 1, 1), built)
+            spot = f * (pitch // 2) + at
+            built = jnp.where(pair == spot, pltpu.roll(bit, 2 * spot + 1, 1), built)
         build[...] = built
 
     def edges(rows, edge):
         count = edge.shape[0]
         lane = lax.broadcasted_iota(jnp.int32, (count, width), 1)
+        pair = lane // 2
+        whole = jnp.zeros((count, width), jnp.float32)
         for f in range(folds):
-            part = slice(f * count, (f + 1) * count)
+            part_rows = slice(f * count, (f + 1) * count)
             built = jnp.zeros((count, width), jnp.float32)
             for x in range(depth):
                 for y in range(height):
-                    row = rows[x + 1, y + 1, part].astype(jnp.float32)
-                    at = f * pitch + x * height + y
-                    built = jnp.where(lane == at, pltpu.roll(row, at, 1), built)
-                    at = at + cells
-                    shift_by = (at + 1) % width
-                    built = jnp.where(lane == at, pltpu.roll(row, shift_by, 1), built)
-            if f == 0:
-                whole = built
-            else:
-                whole = jnp.where(lane < f * pitch, whole, built)
+                    row = rows[x + 1, y + 1, part_rows].astype(jnp.float32)
+                    spot = f * (pitch // 2) + x * height + y
+                    shift_by = (2 * spot + 1) % width
+                    built = jnp.where(pair == spot, pltpu.roll(row, shift_by, 1), built)
+            whole = jnp.where(lane < f * pitch, whole, built)
         edge[...] = whole.astype(edge.dtype)
 
     def shifter():
         src = lax.broadcasted_iota(jnp.int32, (2 * width, 2 * width), 0)
         dst = lax.broadcasted_iota(jnp.int32, (2 * width, 2 * width), 1)
         spot = src % pitch
-        right = jnp.logical_and(src >= width, spot < cells)
-        left = jnp.logical_and(
-            src >= width, jnp.logical_and(spot >= cells, spot < 2 * cells)
-        )
+        used = jnp.logical_and(src >= width, spot < 2 * cells)
+        right = jnp.logical_and(used, spot % 2 == 1)
+        left = jnp.logical_and(used, spot % 2 == 0)
         low = jnp.logical_or(
             jnp.logical_and(src == dst - 1, src < width - 1),
             jnp.logical_and(dst == 0, left),
@@ -320,9 +314,9 @@
                 left = zbuf[0, dx, dy].astype(jnp.float32)
                 right = zbuf[1, dx, dy].astype(jnp.float32)
                 for f in range(folds):
-                    at = f * pitch + (xp - 1) % depth * height + (yp - 1) % height
+                    at = f * pitch + 2 * ((xp - 1) % depth * height + (yp - 1) % height)
                     both = jnp.where(
-                        lane == at, right, jnp.where(lane == cells + at, left, 0.0)
+                        lane == at + 1, right, jnp.where(lane == at, left, 0.0)
                     )
                     halo.append(both.astype(rows.dtype))
             wide = rows[xp, start:end].reshape(span * count, width)
@@ -585,11 +579,11 @@
     for x in range(depth):
         rv[x + 1, 1 : height + 1] = jnp.swapaxes(volume[:, x], 0, 1)
     cells0, cells1, cells2 = (rv, zv, ev, 0), (rp, zp, ep, 1), (rj, zj, ej, 2)
+    edges(rv, ev)
     pl.semaphore_wait(barrier, greeted)
+    send_rest(cells0, True)
+    send_rest(cells0, False)
     send_faces(cells0, 0)
-    send_rest(cells0, False)
-    edges(rv, ev)
-    send_rest(cells0, True)
     send_faces(cells0, 1)
     send_faces(cells0, 2)
     build1[...] = jnp.zeros_like(build1)
@@ -620,8 +614,8 @@
             ep[...] = build1[...].astype(ep.dtype)
         else:
             edges(rp, ep)
+        send_rest(cells1, True)
         send_rest(cells1, False)
-        send_rest(cells1, True)
         send_faces(cells1, 2)
 
     stage(
@@ -653,8 +647,8 @@
             ej[...] = build2[...].astype(ej.dtype)
         else:
             edges(rj, ej)
+        send_rest(cells2, True)
         send_rest(cells2, False)
-        send_rest(cells2, True)
         send_faces(cells2, 1)
 
     stage(
@@ -676,9 +670,9 @@
     correlate(sv, back_ref, 0, 1)
     gather(0)
     gather(1)
+    sent(cells2)
     drain(0, gv2, vs)
     drain(1, gv1, vf)
-    sent(cells2)
 
 
 def place_out(*refs):

time: 39.4 us -> 38.3 us (0.972)
  Pallas kernels: 38.6 us -> 37.5 us
    pallas_call x1, Pallas kernels: 37.5 us -> 36.5 us  [body(): pl.pallas_call(functools.partial(kernel, sizes), out_shape=(jax.ShapeDtyp...]
where the time goes in v7:
time: 38.3 us; the launch traced here: 38.2 us
  Pallas kernels  37.5 us (98%)
  between operations  0.64 us (2%)
    pallas_call x1, Pallas kernels, body(): pl.pallas_call(functools.partial(kernel, sizes), out_shape=(jax.ShapeDtyp...  36.5 us
    pallas_call x1, Pallas kernels, body(): pl.pallas_call(place_out, out_shape=(jax.ShapeDtypeStruct(volume.shape, b...  1.02 us

profile of v7, /device:TPU:0, one launch (start us, length us, event | category | flops | bytes accessed | tf_op | source)
XLA Modules:
  0.0 38.2 jit_solution(9480594265745544101)
XLA Ops:
  0.6 36.5 %shard_map.76 = (bf16[32,2,16,128]{3,2,1,0:T(8,128)(2,1)S(1)}, f32[864,32]{1,0:T(8,128)S(1)}, f32[864,32]{1,0:T(8,128)S(1)}) custom-call(bf16[32,2,16,128]{3,2,1,0:T(8,128)(2,1)} %volume_hbm.1, bf16[864,32]{1,0:T(8,128)(2,1)} %bitcast.6, bf16[864,32]{1,0:T(8,128)(2,1)} %bitcast.7, bf16[864,32]{1,0:T(8,128)(2,1)} %bitcast.8, bf16[864,32]{1,0:T(8,128)(2,1)} %bitcast.9), custom_call_target="tpu_custom_call" | custom-call | tf_op jit(solution)/shard_map/pallas_call | solution.py:701
  37.1 1.0 %shard_map.77 = (bf16[32,2,16,128]{3,2,1,0:T(8,128)(2,1)}, f32[864,32]{1,0:T(8,128)}, f32[864,32]{1,0:T(8,128)}) custom-call(bf16[32,2,16,128]{3,2,1,0:T(8,128)(2,1)S(1)} %get-tuple-element.9.refs_0_, f32[864,32]{1,0:T(8,128)S(1)} %get-tuple-element.10.refs_1_, f32[864,32]{1,0:T(8,128)S(1)} %get-tuple-element.11.refs_2_), custom_call_target="tpu_custom_call" | custom-call | tf_op jit(solution)/shard_map/pallas_call | solution.py:759

commit v8 on v7

--- a/solution.py
+++ b/solution.py
@@ -225,7 +225,8 @@
         rows, zbuf, _, slot = halo
         receive(halo, 0, (0,))
         spread(rows, zbuf, out, near, 0, height + 2)
-        convolve(table, out, group, 0, finish, 0, height // (2 * group))
+        if len(plan) > 1:
+            convolve(table, out, group, 0, finish, 0, height // (2 * group))
         done = 0
         for parts, upto, hook in plan:
             if parts:
@@ -234,7 +235,7 @@
                 end = height + 2 if last == height else last + 1
                 start = 0 if parts[0] == 0 else cuts[slot][parts[0] - 1] + 1
                 spread(rows, zbuf, out, far, start, end)
-            convolve(table, out, group, 1, finish, done, upto)
+            convolve(table, out, group, 1 if len(plan) > 1 else 2, finish, done, upto)
             done = upto
             hook()
 
@@ -348,9 +349,9 @@
 
     def convolve(table, ref, group, kind, finish, lo, hi):
         outs = table.shape[1] // (depth * group)
-        planes = (near, far)[kind]
-
-        @pl.loop(lo, hi, unroll=hi - lo if kind == 0 and table is not t3 else 1)
+        planes = (near, far, near + far)[kind]
+
+        @pl.loop(lo, hi, unroll=1 if kind == 1 else hi - lo)
         def _(j):
             halves = []
             for half in range(2):
@@ -367,13 +368,16 @@
                     )
                 )
             rhs = jnp.concatenate(halves, axis=1)
-            out = jnp.dot(
-                table[kind, :, : rhs.shape[0]], rhs, preferred_element_type=jnp.float32
-            )
+            if kind == 2:
+                weights = jnp.concatenate([table[0], table[1]], axis=1)
+            else:
+                weights = table[kind, :, : rhs.shape[0]]
+            out = jnp.dot(weights, rhs, preferred_element_type=jnp.float32)
             if kind == 0:
                 keep[j] = out
                 return
-            out = out + keep[j]
+            if kind == 1:
+                out = out + keep[j]
             for half in range(2):
                 for ox in range(depth):
                     for oy in range(group):

time: 38.3 us -> 38.2 us (level)
  no operation moved by 1% of the time
where the time goes in v8:
time: 38.2 us; the launch traced here: 38 us
  Pallas kernels  37.4 us (98%)
  between operations  0.64 us (2%)
    pallas_call x1, Pallas kernels, body(): pl.pallas_call(functools.partial(kernel, sizes), out_shape=(jax.ShapeDtyp...  36.3 us
    pallas_call x1, Pallas kernels, body(): pl.pallas_call(place_out, out_shape=(jax.ShapeDtypeStruct(volume.shape, b...  1.02 us

profile of v8, /device:TPU:0, one launch (start us, length us, event | category | flops | bytes accessed | tf_op | source)
XLA Modules:
  0.0 38.0 jit_solution(7840923906084174582)
XLA Ops:
  0.6 36.3 %shard_map.76 = (bf16[32,2,16,128]{3,2,1,0:T(8,128)(2,1)S(1)}, f32[864,32]{1,0:T(8,128)S(1)}, f32[864,32]{1,0:T(8,128)S(1)}) custom-call(bf16[32,2,16,128]{3,2,1,0:T(8,128)(2,1)} %volume_hbm.1, bf16[864,32]{1,0:T(8,128)(2,1)} %bitcast.6, bf16[864,32]{1,0:T(8,128)(2,1)} %bitcast.7, bf16[864,32]{1,0:T(8,128)(2,1)} %bitcast.8, bf16[864,32]{1,0:T(8,128)(2,1)} %bitcast.9), custom_call_target="tpu_custom_call" | custom-call | tf_op jit(solution)/shard_map/pallas_call | solution.py:705
  37.0 1.0 %shard_map.77 = (bf16[32,2,16,128]{3,2,1,0:T(8,128)(2,1)}, f32[864,32]{1,0:T(8,128)}, f32[864,32]{1,0:T(8,128)}) custom-call(bf16[32,2,16,128]{3,2,1,0:T(8,128)(2,1)S(1)} %get-tuple-element.9.refs_0_, f32[864,32]{1,0:T(8,128)S(1)} %get-tuple-element.10.refs_1_, f32[864,32]{1,0:T(8,128)S(1)} %get-tuple-element.11.refs_2_), custom_call_target="tpu_custom_call" | custom-call | tf_op jit(solution)/shard_map/pallas_call | solution.py:763

commit v9 on v8

--- a/solution.py
+++ b/solution.py
@@ -27,7 +27,7 @@
 
 
 def codes(sizes):
-    spans = [3 if size > 2 else 2 for size in sizes]
+    spans = [3 if size > 2 else 2 for size in sizes[:2]]
 
     def code(step):
         total = 0
@@ -67,7 +67,7 @@
     (rv, rp, rj, zv, zp, zj, ev, ep, ej, sv, sp, sj, slope_ref, back_ref,
      t1, t2, t3, shift, keep, prod, diag, pack, land, part, full, told,
      hsend, hrecv, asend, arecv, bsend, brecv,
-     volume, wf, ws, vf, vs, w1, w2, w3, build1, build2, isem) = scratch
+     volume, wf, ws, vf, vs, w1, w2, w3, build1, build2, blank, isem) = scratch
     chan, depth, height, width = volume.shape
     code, ways = codes(sizes)
     early = height - 4
@@ -157,21 +157,23 @@
         return zbuf.at[0 if step[2] == 1 else 1, 1 - step[0], 1 - step[1]]
 
     def message(step, rows, zbuf, edge, slot, piece=None):
-        lane = code(step)
+        lane = take = code(step)
         if step[2] != 0:
             src = edge
+            lane = ways + 4
+            take = lane + (step[0] != 0)
         elif piece is None:
             src = rows.at[source(step[0], depth), source(step[1], height)]
         else:
             part, lo, hi = piece
             src = rows.at[source(step[0], depth), pl.ds(1 + lo, hi - lo)]
             if part:
-                lane = ways + 2 * (part - 1) + (step[0] > 0)
+                lane = take = ways + 2 * (part - 1) + (step[0] > 0)
         return pltpu.make_async_remote_copy(
             src_ref=src,
             dst_ref=landing(step, rows, zbuf, piece),
             send_sem=hsend.at[lane],
-            recv_sem=hrecv.at[slot % 2, lane],
+            recv_sem=hrecv.at[slot % 2, take],
             device_id=tuple(p + d for p, d in zip(me, step)),
             device_id_type=MESH,
         )
@@ -203,11 +205,32 @@
                 ref = landing(step, rows, zbuf)
                 ref[...] = jnp.zeros(ref.shape, ref.dtype)
 
+    def crosswise(halo, sem, kinds):
+        rows_each = halo[2].shape[0] // (chan // folds)
+        beside = [jnp.where(p > 0, 1, 0) + jnp.where(p < n - 1, 1, 0) for p, n in zip(me, sizes)]
+        options = [(0,) if n == 1 else (1,) if n == 2 else (1, 2) for n in sizes]
+        for nx, ny, nz in itertools.product(*options):
+            count = nz * (1 + ny) * sum(nx if kind else 1 for kind in kinds) * rows_each
+            if not count:
+                continue
+            fits = jnp.logical_and(
+                beside[0] == nx, jnp.logical_and(beside[1] == ny, beside[2] == nz)
+            )
+
+            @pl.when(fits)
+            def _():
+                gone = blank.at[pl.ds(0, count)]
+                pltpu.make_async_copy(gone, gone, sem).wait()
+
     def receive(halo, kind, parts):
+        if 0 in parts:
+            crosswise(halo, hrecv.at[halo[3] % 2, ways + 4 + kind], (kind,))
         for step in STEPS:
             if (step[0] != 0) != (kind == 1):
                 continue
             found = pieces(step, halo[3])
+            if step[2] != 0:
+                continue
             if found == [None]:
                 found = found if 0 in parts else []
             else:
@@ -240,7 +263,10 @@
             hook()
 
     def sent(halo):
+        crosswise(halo, hsend.at[ways + 4], (0, 1))
         for step in STEPS:
+            if step[2] != 0:
+                continue
 
             @pl.when(there(step))
             def _():
@@ -738,8 +764,8 @@
             pltpu.VMEM((2, 3, 8, width), bf),
             pltpu.VMEM((2, 9, 3, 8, width), bf),
             pltpu.VMEM(((total - 1) * 3, 8, width), bf),
-            pltpu.SemaphoreType.DMA((ways + 4,)),
-            pltpu.SemaphoreType.DMA((2, ways + 4)),
+            pltpu.SemaphoreType.DMA((ways + 5,)),
+            pltpu.SemaphoreType.DMA((2, ways + 6)),
             pltpu.SemaphoreType.DMA((2,)),
             pltpu.SemaphoreType.DMA((2, 3)),
             pltpu.SemaphoreType.DMA((2,)),
@@ -754,6 +780,7 @@
             pltpu.VMEM((chan, filt), bf),
             pltpu.VMEM((2 * chan // folds, width), f32),
             pltpu.VMEM((chan // folds, width), f32),
+            pltpu.VMEM((36, chan // folds, width), bf),
             pltpu.SemaphoreType.DMA((5,)),
         ],
         compiler_params=pltpu.CompilerParams(

time: 38.2 us -> 37.8 us (0.990)
  Pallas kernels: 37.4 us -> 37 us
    pallas_call x1, Pallas kernels: 36.3 us -> 35.9 us  [body(): pl.pallas_call(functools.partial(kernel, sizes), out_shape=(jax.ShapeDtyp...]
where the time goes in v9:
time: 37.8 us; the launch traced here: 37.6 us
  Pallas kernels  37 us (98%)
  between operations  0.64 us (2%)
    pallas_call x1, Pallas kernels, body(): pl.pallas_call(functools.partial(kernel, sizes), out_shape=(jax.ShapeDtyp...  35.9 us
    pallas_call x1, Pallas kernels, body(): pl.pallas_call(place_out, out_shape=(jax.ShapeDtypeStruct(volume.shape, b...  1.02 us

profile of v9, /device:TPU:0, one launch (start us, length us, event | category | flops | bytes accessed | tf_op | source)
XLA Modules:
  0.0 37.6 jit_solution(7698428036046262214)
XLA Ops:
  0.6 35.9 %shard_map.76 = (bf16[32,2,16,128]{3,2,1,0:T(8,128)(2,1)S(1)}, f32[864,32]{1,0:T(8,128)S(1)}, f32[864,32]{1,0:T(8,128)S(1)}) custom-call(bf16[32,2,16,128]{3,2,1,0:T(8,128)(2,1)} %volume_hbm.1, bf16[864,32]{1,0:T(8,128)(2,1)} %bitcast.6, bf16[864,32]{1,0:T(8,128)(2,1)} %bitcast.7, bf16[864,32]{1,0:T(8,128)(2,1)} %bitcast.8, bf16[864,32]{1,0:T(8,128)(2,1)} %bitcast.9), custom_call_target="tpu_custom_call" | custom-call | tf_op jit(solution)/shard_map/pallas_call | solution.py:731
  36.6 1.0 %shard_map.77 = (bf16[32,2,16,128]{3,2,1,0:T(8,128)(2,1)}, f32[864,32]{1,0:T(8,128)}, f32[864,32]{1,0:T(8,128)}) custom-call(bf16[32,2,16,128]{3,2,1,0:T(8,128)(2,1)S(1)} %get-tuple-element.9.refs_0_, f32[864,32]{1,0:T(8,128)S(1)} %get-tuple-element.10.refs_1_, f32[864,32]{1,0:T(8,128)S(1)} %get-tuple-element.11.refs_2_), custom_call_target="tpu_custom_call" | custom-call | tf_op jit(solution)/shard_map/pallas_call | solution.py:790

commit v10 on v9

--- a/solution.py
+++ b/solution.py
@@ -563,6 +563,7 @@
             finish_tile(slot, extra_at * batch + len(base), 0, len(base), extra_at)
 
     def drain(slot, out, direction):
+        out[...] = (0.1 * factor) * direction[...].astype(jnp.float32)
         none = jnp.logical_not(jnp.logical_or(is_base, is_extra))
         for owned, here in ((3, is_base), (1, is_extra), (0, none)):
 
@@ -580,9 +581,7 @@
             whole = full[slot, :, kx].astype(jnp.float32).reshape(step_rows, width)
             for j in range(lanes):
                 at = slice(kx * slab + j * step_rows, kx * slab + (j + 1) * step_rows)
-                damp = 0.1 * direction[at].astype(jnp.float32)
-                mean = whole[:, j * chan : (j + 1) * chan] * (1.0 / cells_all)
-                out[at] = factor * (mean + damp)
+                out[at] += whole[:, j * chan : (j + 1) * chan] * (factor / cells_all)
 
     def arrange():
         filt = 27 * chan

time: 37.8 us -> 37.6 us (level)
  no operation moved by 1% of the time
where the time goes in v10:
time: 37.6 us; the launch traced here: 37.4 us
  Pallas kernels  36.8 us (98%)
  between operations  0.64 us (2%)
    pallas_call x1, Pallas kernels, body(): pl.pallas_call(functools.partial(kernel, sizes), out_shape=(jax.ShapeDtyp...  35.7 us
    pallas_call x1, Pallas kernels, body(): pl.pallas_call(place_out, out_shape=(jax.ShapeDtypeStruct(volume.shape, b...  1.02 us

profile of v10, /device:TPU:0, one launch (start us, length us, event | category | flops | bytes accessed | tf_op | source)
XLA Modules:
  0.0 37.4 jit_solution(15880577405315917757)
XLA Ops:
  0.6 35.7 %shard_map.76 = (bf16[32,2,16,128]{3,2,1,0:T(8,128)(2,1)S(1)}, f32[864,32]{1,0:T(8,128)S(1)}, f32[864,32]{1,0:T(8,128)S(1)}) custom-call(bf16[32,2,16,128]{3,2,1,0:T(8,128)(2,1)} %volume_hbm.1, bf16[864,32]{1,0:T(8,128)(2,1)} %bitcast.6, bf16[864,32]{1,0:T(8,128)(2,1)} %bitcast.7, bf16[864,32]{1,0:T(8,128)(2,1)} %bitcast.8, bf16[864,32]{1,0:T(8,128)(2,1)} %bitcast.9), custom_call_target="tpu_custom_call" | custom-call | tf_op jit(solution)/shard_map/pallas_call | solution.py:730
  36.4 1.0 %shard_map.77 = (bf16[32,2,16,128]{3,2,1,0:T(8,128)(2,1)}, f32[864,32]{1,0:T(8,128)}, f32[864,32]{1,0:T(8,128)}) custom-call(bf16[32,2,16,128]{3,2,1,0:T(8,128)(2,1)S(1)} %get-tuple-element.9.refs_0_, f32[864,32]{1,0:T(8,128)S(1)} %get-tuple-element.10.refs_1_, f32[864,32]{1,0:T(8,128)S(1)} %get-tuple-element.11.refs_2_), custom_call_target="tpu_custom_call" | custom-call | tf_op jit(solution)/shard_map/pallas_call | solution.py:789
